TPU v7x, 8 devices: a whole 2x2x1 slice. The times are simulated.
8 devices in a mesh: dp: 1 (over z), ep: 8 (over y, x, core).
Axes of the slice: x: 2, y: 2, z: 1, core: 2. Of those that a mesh axis runs over, the one named last changes fastest.
Arguments:
- tokens: bfloat16 [32768, 1536], P(('dp', 'ep'))
- routes: int32 [32768, 8], P(('dp', 'ep'))
- w_router: bfloat16 [1536, 40], replicated
- w_one: bfloat16 [40, 1536, 512], P('ep')
- w_three: bfloat16 [40, 1536, 512], P('ep')
- w_two: bfloat16 [40, 512, 1536], P('ep')
Outputs:
- output: bfloat16 [32768, 1536], P(('dp', 'ep'))
All inputs are finite; a program needn't handle non-finite values.
Results may differ from a plain program's by a relative error of at most 0.00818649.
Values are sent between devices in bfloat16 or wider.
A program may use at most 1 GiB of HBM per device.

v0:
```python
import jax
import jax.numpy as jnp
from jax import lax
from jax.sharding import PartitionSpec as P


def slot_capacity(num_tokens, top_k, num_experts):
    return 8 * ((3 * num_tokens * top_k + 16 * num_experts - 1) // (16 * num_experts))


def route_gates(tokens, routes, w_router):
    logits = jnp.dot(tokens, w_router, preferred_element_type=jnp.float32)
    return jax.nn.softmax(jnp.take_along_axis(logits, routes, axis=1), axis=-1)


def dispatch_plan(routes, num_experts, capacity):
    top_k = routes.shape[1]
    flat_routes = routes.reshape(-1)
    num_pairs = flat_routes.shape[0]
    sort_order = jnp.argsort(flat_routes, stable=True)
    counts = jax.ops.segment_sum(jnp.ones_like(flat_routes), flat_routes, num_segments=num_experts)
    starts = jnp.cumsum(counts) - counts
    slot_ids = starts[:, None] + jnp.arange(capacity, dtype=jnp.int32)[None, :]
    token_at = sort_order[jnp.minimum(slot_ids, num_pairs - 1)] // top_k
    pair_rank = jnp.zeros_like(sort_order).at[sort_order].set(jnp.arange(num_pairs, dtype=sort_order.dtype))
    pair_row = flat_routes * capacity + pair_rank - starts[flat_routes]
    return token_at, pair_row


def expert_mlp(rows, w_one, w_three, w_two):
    gate_pre = jnp.einsum('erd,edf->erf', rows, w_one, preferred_element_type=jnp.float32)
    up_pre = jnp.einsum('erd,edf->erf', rows, w_three, preferred_element_type=jnp.float32)
    hidden = (jax.nn.silu(gate_pre) * up_pre).astype(jnp.bfloat16)
    return jnp.einsum('erf,efd->erd', hidden, w_two, preferred_element_type=jnp.float32).astype(jnp.bfloat16)


def solution(mesh):
    group_size = mesh.shape['ep']
    row_spec = P(('dp', 'ep'), None)
    expert_spec = P('ep', None, None)

    def device_step(tokens, routes, w_router, w_one, w_three, w_two):
        num_tokens, d_model = tokens.shape
        top_k = routes.shape[1]
        num_experts = w_router.shape[1]
        local_experts = w_one.shape[0]
        capacity = slot_capacity(num_tokens, top_k, num_experts)
        gate_vals = route_gates(tokens, routes, w_router)
        token_at, pair_row = dispatch_plan(routes, num_experts, capacity)
        send_rows = tokens[token_at].reshape(num_experts, 1, capacity, d_model)
        recv_rows = lax.all_to_all(send_rows, 'ep', 0, 1, tiled=True)
        out_rows = expert_mlp(recv_rows.reshape(local_experts, group_size * capacity, d_model), w_one, w_three, w_two)
        back_rows = lax.all_to_all(out_rows.reshape(local_experts, group_size, capacity, d_model), 'ep', 1, 0, tiled=True)
        pair_out = back_rows.reshape(num_experts * capacity, d_model)[pair_row].reshape(num_tokens, top_k, d_model)
        return jnp.sum(gate_vals[:, :, None] * pair_out, axis=1).astype(jnp.bfloat16)

    return jax.shard_map(device_step, mesh=mesh, in_specs=(row_spec, row_spec, P(None, None), expert_spec, expert_spec, expert_spec), out_specs=row_spec, check_vma=False)
```

profile of v0, /device:TPU:0, one launch (start us, length us, event | category | flops | bytes accessed | tf_op | source)
XLA Modules:
  0.0 5353.8 jit_solution(4832449167450856220)
XLA Ops:
  0.0 1.5 copy.34
  1.6 1.1 reshape.205
  2.7 226.8 %scatter_custom_fusion = s32[40]{0:T(128)S(1)} fusion(s32[32768]{0:T(1024)S(1)} %reshape.205, s32[32768]{0:T(1024)S(1)} %broadcast.249, s32[]{:T(128)} %constant.17.clone.1), kind=kCustom, calls=%fused_computation.75 | custom fusion | flops 32768 | bytes 164 | tf_op jit(solution)/shard_map/scatter-add | solution.py:21
  229.8 11.1 sort.17
  241.3 252.5 %gather_fusion = s32[49280]{0:T(1024)S(1)} fusion(s32[32768]{0:T(1024)S(1)} %get-tuple-element.6, s32[50176]{0:T(1024)S(1)} %pad_clamp_fusion.1), kind=kCustom, calls=%fused_computation | custom fusion | bytes 591360 | tf_op jit(solution)/shard_map/gather | solution.py:24
  494.4 296.3 %gather_fusion.1 = bf16[49280,1536]{1,0:T(8,128)(2,1)} fusion(bf16[4096,1536]{1,0:T(8,128)(2,1)} %param.6, s32[50176]{0:T(1024)S(1)} %pad_clamp_fusion), kind=kCustom, calls=%fused_computation.1 | custom fusion | bytes 302973440 | tf_op jit(solution)/shard_map/gather | solution.py:50
  790.7 1662.5 %all_to_all.30 = bf16[40,1,1232,1536]{3,2,1,0:T(8,128)(2,1)} all-to-all(bf16[40,1,1232,1536]{3,2,1,0:T(8,128)(2,1)} %bitcast.3), channel_id=1, replica_groups=mesh['dp'=1,'ep'=8] {'ep'}, dimensions={0} | all-to-all | bytes 302776320 | tf_op jit(solution)/shard_map/all_to_all | solution.py:51
  2453.2 99.4 %copy.37 = bf16[5,8,1,1232,1536]{4,3,1,0,2:T(8,128)(2,1)} copy(bf16[5,8,1,1232,1536]{4,3,0,1,2:T(8,128)(2,1)} %bitcast.5) | data formatting | bytes 302776320 | tf_op jit(solution)/shard_map/all_to_all | solution.py:51
  2552.6 95.9 %fusion.19 = f32[5,9856,512]{2,1,0:T(8,128)} fusion(bf16[5,9856,1536]{2,1,0:T(8,128)(2,1)} %bitcast.6, bf16[5,1536,512]{2,1,0:T(8,128)(2,1)} %param.9), kind=kOutput, calls=%fused_computation.83 | convolution fusion | flops 77510737920 | bytes 260177920 | tf_op jit(solution)/shard_map/erd,edf->erf/dot_general | solution.py:31
  2648.5 180.9 %convolution_convert_fusion = bf16[5,9856,1536]{2,1,0:T(8,128)(2,1)} fusion(bf16[5,512,1536]{2,1,0:T(8,128)(2,1)} %param.11, f32[5,9856,512]{2,1,0:T(8,128)} %fusion.19, bf16[5,9856,1536]{2,1,0:T(8,128)(2,1)} %bitcast.6, bf16[5,1536,512]{2,1,0:T(8,128)(2,1)} %param.10), kind=kOutput, calls=%fused_computation.8 | convolution fusion | flops 155248558080 | bytes 419430400 | tf_op jit(solution)/shard_map/erf,efd->erd/dot_general | solution.py:34
  2829.4 99.6 %copy.38 = bf16[5,8,1232,1536]{3,2,0,1:T(8,128)(2,1)} copy(bf16[5,8,1232,1536]{3,2,1,0:T(8,128)(2,1)} %bitcast.7) | data formatting | bytes 302776320 | tf_op jit(solution)/shard_map/reshape | solution.py:53
  2929.0 13.9 all-to-all-start.1
  2942.9 1.7 broadcast_in_dim_reshape.3
  2946.3 8.3 fusion.18
  2954.7 260.6 %gather_fusion.3 = f32[32768]{0:T(1024)S(1)} fusion(f32[4096,40]{0,1:T(8,128)S(1)} %fusion.18, s32[32768]{0:T(1024)S(1)} %reshape.284), kind=kCustom, calls=%fused_computation.3 | custom fusion | bytes 524288 | tf_op jit(solution)/shard_map/jit(take_along_axis)/gather | solution.py:13
  3215.3 1.1 reshape.287
  3217.2 1.9 copy.33
  3219.2 120.1 %scatter_custom_fusion.1 = s32[32768]{0:T(1024)S(1)} fusion(s32[32768]{0:T(1024)S(1)} %compare_select_fusion.10, s32[32768]{0:T(1024)S(1)} %iota.14, s32[]{:T(128)} %constant.17.clone.1), kind=kCustom, calls=%fused_computation.73 | custom fusion | bytes 131076 | tf_op jit(solution)/shard_map/scatter | solution.py:25
  3341.4 4.9 compare_select_fusion.3
  3346.3 16.0 compare_reduce_fusion.32
  3362.3 20.8 fusion.6
  3383.2 1187.4 %all-to-all-done.1 = bf16[5,8,1232,1536]{3,2,0,1:T(8,128)(2,1)} async-done(((bf16[5,8,1232,1536]{3,2,0,1:T(8,128)(2,1)}), bf16[5,8,1232,1536]{3,2,0,1:T(8,128)(2,1)}, u32[]{:S(2)}, u32[]{:S(2)}) %all-to-all-start.1) | async-done | bytes 151388192 | tf_op jit(solution)/shard_map/all_to_all | solution.py:53
  4570.6 698.8 %gather_fusion.2 = bf16[32768,1536]{1,0:T(8,128)(2,1)} fusion(bf16[49280,1536]{1,0:T(8,128)(2,1)} %bitcast.10, s32[32768]{0:T(1024)S(1)} %fusion.6), kind=kCustom, calls=%fused_computation.2 | custom fusion | bytes 201457664 | tf_op jit(solution)/shard_map/gather | solution.py:54
  5269.3 84.0 %fusion = bf16[4096,1536]{1,0:T(8,128)(2,1)} fusion(bf16[32768,1536]{1,0:T(8,128)(2,1)} %gather_fusion.2, f32[4096,8]{1,0:T(8,128)S(1)} %copy-done.5), kind=kLoop, calls=%fused_computation.7 | loop fusion | flops 144703488 | bytes 113377280 | tf_op jit(solution)/shard_map/reduce_sum | solution.py:55
  (51 shorter events, 5.8 us)
Async XLA Ops:
  0.0 2946.3 %copy-start = (bf16[1536,40]{0,1:T(8,128)(2,1)S(1)}, bf16[1536,40]{0,1:T(8,128)(2,1)}, u32[]{:S(2)}) copy-start(bf16[1536,40]{0,1:T(8,128)(2,1)} %param.8) | copy-start | bytes 368644
  1.5 228.2 %copy-start.3 = (s32[4096,8]{1,0:T(8,128)}, s32[4096,8]{1,0:T(8,128)S(1)}, u32[]{:S(2)}) copy-start(s32[4096,8]{1,0:T(8,128)S(1)} %copy.34) | copy-start | bytes 393220
  2.6 491.2 %copy-start.8 = (s32[32768]{0:T(1024)}, s32[32768]{0:T(1024)S(1)}, u32[]{:S(2)}) copy-start(s32[32768]{0:T(1024)S(1)} %reshape.205) | copy-start | bytes 393220
  229.8 264.1 %copy-start.10 = (s32[40]{0:T(128)}, s32[40]{0:T(128)S(1)}, u32[]{:S(2)}) copy-start(s32[40]{0:T(128)S(1)} %sub.24) | copy-start | bytes 484
  241.0 252.9 %copy-start.1 = (s32[32768]{0:T(1024)}, s32[32768]{0:T(1024)S(1)}, u32[]{:S(2)}) copy-start(s32[32768]{0:T(1024)S(1)} %get-tuple-element.6) | copy-start | bytes 393220
  2929.0 13.9 copy-start.4
  2929.0 15.6 copy-start.6
  2929.0 1641.6 %all-to-all-start.1 = ((bf16[5,8,1232,1536]{3,2,0,1:T(8,128)(2,1)}), bf16[5,8,1232,1536]{3,2,0,1:T(8,128)(2,1)}, u32[]{:S(2)}, u32[]{:S(2)}) async-start(bf16[5,8,1232,1536]{3,2,0,1:T(8,128)(2,1)} %copy.38), calls=%async_computation.1 | async-start | bytes 302776320 | tf_op jit(solution)/shard_map/all_to_all | solution.py:53
  2954.6 262.4 %copy-start.7 = (s32[4096,8]{0,1:T(8,128)S(1)}, s32[4096,8]{0,1:T(8,128)}, u32[]{:S(2)}) copy-start(s32[4096,8]{0,1:T(8,128)} %param.7) | copy-start | bytes 393220
  2954.6 264.5 %copy-start.2 = (s32[32768]{0:T(1024)S(1)}, s32[32768]{0:T(1024)}, u32[]{:S(2)}) copy-start(s32[32768]{0:T(1024)} %copy-done.1) | copy-start | bytes 393220
  2954.7 384.6 %copy-start.11 = (s32[40]{0:T(128)S(1)}, s32[40]{0:T(128)}, u32[]{:S(2)}) copy-start(s32[40]{0:T(128)} %copy-done.10) | copy-start | bytes 484
  2954.7 386.8 %copy-start.12 = (s32[32768,1]{0,1:T(1,128)S(1)}, s32[32768,1]{0,1:T(1,128)}, u32[]{:S(2)}) copy-start(s32[32768,1]{0,1:T(1,128)} %broadcast_in_dim_reshape.3) | copy-start | bytes 393220
  2954.7 407.7 %copy-start.9 = (s32[32768]{0:T(1024)S(1)}, s32[32768]{0:T(1024)}, u32[]{:S(2)}) copy-start(s32[32768]{0:T(1024)} %copy-done.8) | copy-start | bytes 393220
  4570.6 698.8 %copy-start.5 = (f32[4096,8]{1,0:T(8,128)S(1)}, f32[4096,8]{1,0:T(8,128)}, u32[]{:S(2)}) copy-start(f32[4096,8]{1,0:T(8,128)} %copy.33) | copy-start | bytes 393220
where the time goes:
time: 5370 us; the launch traced here: 5350 us
  local copies, waits for them, and re-layouts  1840 us (34%)
  blocking collectives  1660 us (31%)
  waiting for transfers between devices  1190 us (22%)
  other arithmetic  365 us (7%)
  matrix products  285 us (5%)
    all_to_all x1, blocking collectives, device_step(): recv_rows = lax.all_to_all(send_rows, 'ep', 0, 1, tiled=True)  1660 us
    all_to_all x1, waiting for transfers between devices, device_step(): lax.all_to_all(out_rows.reshape(local_experts, group_size, capacity, d_mo...  1190 us
    gather x1, local copies, waits for them, and re-layouts, device_step(): back_rows.reshape(num_experts * capacity, d_model)[pair_row]  699 us
    gather x1, local copies, waits for them, and re-layouts, device_step(): send_rows = tokens[token_at].reshape(num_experts, 1, capacity, d_model)  296 us
    gather x5, local copies, waits for them, and re-layouts, route_gates(): return jax.nn.softmax(jnp.take_along_axis(logits, routes, axis=1), axis=-1)  264 us
    gather x2, local copies, waits for them, and re-layouts, dispatch_plan(): token_at = sort_order[jnp.minimum(slot_ids, num_pairs - 1)] // top_k  253 us
    scatter-add x1, other arithmetic, dispatch_plan(): jax.ops.segment_sum(jnp.ones_like(flat_routes), flat_routes, num_segments...  227 us
    dot_general x1, matrix products, expert_mlp(): jnp.einsum('erf,efd->erd', hidden, w_two, preferred_element_type=jnp.floa...  181 us
  transfers between devices with their start and end apart: 1, of which 1 were waited for; matrix products, arithmetic and copies ran while one was open for 8% of the time, Pallas kernels for 0%

commit v1 on v0

v1 whole, which is shorter than its diff:
```python
import functools

import jax
import jax.numpy as jnp
from jax import lax
from jax.experimental import pallas as pl
from jax.experimental.pallas import tpu as pltpu
from jax.sharding import PartitionSpec as P

LANES = 128
SUBLANES = 8
TILE = 256
UNROLL = 8


def route_lists(tokens, routes, w_router):
    num_tokens, top_k = routes.shape
    num_experts = w_router.shape[1]
    chunks = tokens.shape[1] // LANES
    logits = jnp.dot(tokens, w_router, preferred_element_type=jnp.float32).T
    slots = routes.T
    experts = jnp.arange(num_experts, dtype=jnp.int32)
    hit = slots[:, None, :] == experts[None, :, None]
    picked = jnp.sum(jnp.where(hit, logits[None], 0.0), axis=1)
    gates = jax.nn.softmax(picked, axis=0)
    counts = jnp.sum(hit, axis=(0, 2), dtype=jnp.int32)
    starts = jnp.cumsum(counts) - counts
    keys = slots * num_tokens + jnp.arange(num_tokens, dtype=jnp.int32)[None, :]
    keys, gates = lax.sort((keys.reshape(-1), gates.reshape(-1)), num_keys=1, is_stable=False)
    token_at = keys % num_tokens
    address = (token_at // SUBLANES) * (SUBLANES * chunks) + token_at % SUBLANES
    return jnp.pad(address, (0, TILE)), jnp.pad(gates, (0, TILE)), starts, counts


def to_tiles(rows):
    num_rows, width = rows.shape
    tiled = rows.reshape(num_rows // SUBLANES, SUBLANES, width // LANES, LANES)
    return tiled.transpose(0, 2, 1, 3).reshape(num_rows * (width // LANES), LANES)


def stage_kernel(first, last, num_stage, d_model, starts, counts, address, gates, x_hbm, *refs):
    if first:
        w_one, w_three, w_two, out, x_v, y_v, one_v, three_v, two_v, rows_v, outs_v, cast_v, w_sem, io_sem = refs
        y_hbm = None
    else:
        y_hbm, w_one, w_three, w_two, out, x_v, y_v, one_v, three_v, two_v, rows_v, outs_v, cast_v, w_sem, io_sem = refs
    chunks = d_model // LANES

    def weight_copies(e):
        slot = lax.rem(e, 2)
        return [
            pltpu.make_async_copy(src.at[e], dst.at[slot], w_sem.at[slot, i])
            for i, (src, dst) in enumerate(((w_one, one_v), (w_three, three_v), (w_two, two_v)))
        ]

    x_copy = pltpu.make_async_copy(x_hbm, x_v, io_sem.at[0])
    x_copy.start()
    for copy in weight_copies(0):
        copy.start()
    if first:
        def clear(i, _):
            y_v[pl.ds(pl.multiple_of(i * 256, 256), 256), :] = jnp.zeros((256, LANES), jnp.float32)
            return 0
        lax.fori_loop(0, y_v.shape[0] // 256, clear, 0)
    else:
        y_copy = pltpu.make_async_copy(y_hbm, y_v, io_sem.at[1])
        y_copy.start()
        y_copy.wait()
    x_copy.wait()

    def row_slice(base):
        return pl.ds(base, chunks, stride=SUBLANES)

    def expert(e, _):
        slot = lax.rem(e, 2)

        @pl.when(e + 1 < num_stage)
        def _():
            for copy in weight_copies(e + 1):
                copy.start()

        for copy in weight_copies(e):
            copy.wait()
        begin = starts[e]
        count = counts[e]

        def tile(t, _):
            tile_begin = begin + t * TILE
            live = jnp.minimum(count - t * TILE, TILE)

            def gather(g, _):
                at = tile_begin + g * SUBLANES
                rows = [x_v[row_slice(address[at + u]), :] for u in range(SUBLANES)]
                for u in range(SUBLANES):
                    rows_v[row_slice(g * (SUBLANES * chunks) + u), :] = rows[u]
                return 0

            lax.fori_loop(0, TILE // SUBLANES, gather, 0)
            tiled = rows_v[...].reshape(TILE // SUBLANES, chunks, SUBLANES, LANES)
            lhs = jnp.concatenate([tiled[:, c].reshape(TILE, LANES).astype(jnp.bfloat16) for c in range(chunks)], axis=1)
            gate_pre = jnp.dot(lhs, one_v[slot], preferred_element_type=jnp.float32)
            up_pre = jnp.dot(lhs, three_v[slot], preferred_element_type=jnp.float32)
            hidden = (jax.nn.silu(gate_pre) * up_pre).astype(jnp.bfloat16)
            down = jnp.dot(hidden, two_v[slot], preferred_element_type=jnp.float32)
            down = down.astype(jnp.bfloat16).astype(jnp.float32)
            parts = [down[:, c * LANES:(c + 1) * LANES].reshape(TILE // SUBLANES, 1, SUBLANES, LANES) for c in range(chunks)]
            outs_v[...] = jnp.concatenate(parts, axis=1).reshape(TILE * chunks, LANES)

            def add_rows(first_row, size, local):
                at = [tile_begin + first_row + u for u in range(size)]
                where = [address[a] for a in at]
                sums = [y_v[row_slice(w), :] for w in where]
                terms = [outs_v[row_slice(local + u), :] * gates[a] for u, a in enumerate(at)]
                for u in range(size):
                    y_v[row_slice(where[u]), :] = sums[u] + terms[u]

            def scatter(g, _):
                add_rows(g * SUBLANES, SUBLANES, g * (SUBLANES * chunks))
                return 0

            full = live // SUBLANES
            lax.fori_loop(0, full, scatter, 0)

            def scatter_one(r, _):
                add_rows(full * SUBLANES + r, 1, full * (SUBLANES * chunks) + r)
                return 0

            lax.fori_loop(0, live - full * SUBLANES, scatter_one, 0)
            return 0

        lax.fori_loop(0, (count + TILE - 1) // TILE, tile, 0)
        return 0

    lax.fori_loop(0, num_stage, expert, 0)

    if last:
        block = cast_v.shape[1]
        steps = (y_v.shape[0] // chunks) // block

        def out_copy(i):
            return pltpu.make_async_copy(cast_v.at[lax.rem(i, 2)], out.at[pl.ds(pl.multiple_of(i * block, block), block)], io_sem.at[lax.rem(i, 2)])

        def finish(i, _):
            @pl.when(i >= 2)
            def _():
                out_copy(i - 2).wait()
            part = y_v[pl.ds(pl.multiple_of(i * (block * chunks), block * chunks), block * chunks), :].reshape(block // SUBLANES, chunks, SUBLANES, LANES)
            cast_v[lax.rem(i, 2)] = jnp.concatenate([part[:, c].reshape(block, LANES).astype(jnp.bfloat16) for c in range(chunks)], axis=1)
            out_copy(i).start()
            return 0

        lax.fori_loop(0, steps, finish, 0)
        out_copy(steps - 2).wait()
        out_copy(steps - 1).wait()
    else:
        out_copy = pltpu.make_async_copy(y_v, out, io_sem.at[0])
        out_copy.start()
        out_copy.wait()


def run_stage(x_tiles, y_tiles, starts, counts, address, gates, w_one, w_three, w_two, last):
    num_stage, d_model, d_expert = w_one.shape
    chunks = d_model // LANES
    num_rows = x_tiles.shape[0] // chunks
    first = y_tiles is None
    smem = pl.BlockSpec(memory_space=pltpu.SMEM)
    hbm = pl.BlockSpec(memory_space=pl.ANY)
    arrays = [x_tiles] + ([] if first else [y_tiles]) + [w_one, w_three, w_two]
    if last:
        out_shape = jax.ShapeDtypeStruct((num_rows, d_model), jnp.bfloat16)
    else:
        out_shape = jax.ShapeDtypeStruct(x_tiles.shape, jnp.float32)
    return pl.pallas_call(
        functools.partial(stage_kernel, first, last, num_stage, d_model),
        out_shape=out_shape,
        in_specs=[smem] * 4 + [hbm] * len(arrays),
        out_specs=hbm,
        scratch_shapes=[
            pltpu.VMEM(x_tiles.shape, jnp.float32),
            pltpu.VMEM(x_tiles.shape, jnp.float32),
            pltpu.VMEM((2, d_model, d_expert), jnp.bfloat16),
            pltpu.VMEM((2, d_model, d_expert), jnp.bfloat16),
            pltpu.VMEM((2, d_expert, d_model), jnp.bfloat16),
            pltpu.VMEM((TILE * chunks, LANES), jnp.float32),
            pltpu.VMEM((TILE * chunks, LANES), jnp.float32),
            pltpu.VMEM((2, 64, d_model), jnp.bfloat16),
            pltpu.SemaphoreType.DMA((2, 3)),
            pltpu.SemaphoreType.DMA((2,)),
        ],
        input_output_aliases={} if first or last else {5: 0},
        compiler_params=pltpu.CompilerParams(vmem_limit_bytes=67_043_328),
        cost_estimate=pl.CostEstimate(flops=num_stage * 820 * 6 * d_model * d_expert, bytes_accessed=num_stage * 6 * d_model * d_expert, transcendentals=0),
        name=f"experts_{num_stage}",
    )(starts, counts, address, gates, *arrays)


def solution(mesh):
    row_spec = P(("dp", "ep"), None)
    expert_spec = P("ep", None, None)

    def device_step(tokens, routes, w_router, w_one, w_three, w_two):
        address, gates, starts, counts = route_lists(tokens, routes, w_router)
        x_tiles = to_tiles(tokens.astype(jnp.float32))
        full = [lax.all_gather(w, "ep", axis=0, tiled=True) for w in (w_one, w_three, w_two)]
        return run_stage(x_tiles, None, starts, counts, address, gates, *full, last=True)

    return jax.shard_map(device_step, mesh=mesh, in_specs=(row_spec, row_spec, P(None, None), expert_spec, expert_spec, expert_spec), out_specs=row_spec, check_vma=False)
```

time: 5370 us -> 1300 us (0.24)
  local copies, waits for them, and re-layouts: 1840 us -> 1.48 us
  blocking collectives: 1660 us -> 0 us
  Pallas kernels: 0 us -> 435 us
  waiting for transfers between devices: 1190 us -> 812 us
  other arithmetic: 365 us -> 25.3 us
  matrix products: 285 us -> 8.3 us
    all_to_all x1 -> x0, blocking collectives: 1660 us -> none  [device_step(): recv_rows = lax.all_to_all(send_rows, 'ep', 0, 1, tiled=True)]
    gather x12 -> x0, local copies, waits for them, and re-layouts: 1510 us -> none  [the longest x1 699 us: device_step(): back_rows.reshape(num_experts * capacity, d_model)[pair_row]]
    all_to_all x1 -> x0, waiting for transfers between devices: 1190 us -> none  [device_step(): lax.all_to_all(out_rows.reshape(local_experts, group_size, capacity, d_mo...]
    all_gather x0 -> x3, waiting for transfers between devices: none -> 810 us  [device_step(): lax.all_gather(w, 'ep', axis=0, tiled=True)]
    pallas_call x0 -> x1, Pallas kernels: none -> 435 us  [run_stage(): pl.pallas_call(functools.partial(stage_kernel, first, last, num_stage, d_...]
    dot_general x3 -> x1, matrix products: 285 us -> 8.3 us  [route_lists(): logits = jnp.dot(tokens, w_router, preferred_element_type=jnp.float32).T]
    scatter-add x1 -> x0, other arithmetic: 227 us -> none  [dispatch_plan(): jax.ops.segment_sum(jnp.ones_like(flat_routes), flat_routes, num_segments...]
    scatter x1 -> x0, local copies, waits for them, and re-layouts: 120 us -> none  [dispatch_plan(): jnp.zeros_like(sort_order).at[sort_order]]
  transfers between devices with their start and end apart: 1 -> 3, of which waited for: 1 -> 3; matrix products, arithmetic and copies ran while one was open for 8% -> 3% of each run, Pallas kernels for 0% -> 0%
where the time goes in v1:
time: 1300 us
  waiting for transfers between devices  812 us (62%)
  Pallas kernels  435 us (33%)
  other arithmetic  25.3 us (2%)
  between operations  13.2 us (1%)
    all_gather x3, waiting for transfers between devices, device_step(): lax.all_gather(w, 'ep', axis=0, tiled=True)  810 us
    pallas_call x1, Pallas kernels, run_stage(): pl.pallas_call(functools.partial(stage_kernel, first, last, num_stage, d_...  435 us
  transfers between devices with their start and end apart: 3, of which 3 were waited for; matrix products, arithmetic and copies ran while one was open for 3% of the time, Pallas kernels for 0%

profile of v1, /device:TPU:0, one launch (start us, length us, event | category | flops | bytes accessed | tf_op | source)
XLA Modules:
  0.0 1295.4 jit_solution(1702627170957365580)
XLA Ops:
  6.5 0.7 all-gather.4.cloned.1.call-update
  7.3 0.0 copy-start
  7.3 0.0 copy-start.1
  7.3 0.0 all-gather.6.cloned.1.call-start
  7.3 0.7 all-gather.6.cloned.1.call-update
  8.0 0.0 all-gather.8.cloned.1.call-start
  8.1 0.7 all-gather.8.cloned.1.call-update
  8.8 0.6 convert_reduce_fusion.counts
  9.4 0.1 copy.10
  9.5 0.1 reduce-window.9
  9.5 0.1 reduce
  9.7 0.6 sub.19.starts
  10.3 8.3 fusion.8
  18.6 1.0 select_reduce_fusion
  19.6 0.1 fusion.7
  19.7 7.8 sort.15
  27.6 0.2 fusion.2
  27.7 0.7 pad.8.address
  28.4 0.7 pad.9.gates
  29.1 14.9 %bitcast_convert_fusion = f32[512,8,12,128]{3,1,2,0:T(8,128)} fusion(bf16[4096,1536]{1,0:T(8,128)(2,1)} %param.6), kind=kLoop, calls=%fused_computation | loop fusion | flops 6291456 | bytes 37748736 | tf_op jit(solution)/shard_map/reshape | solution.py:38
  43.9 247.5 %all-gather.4.cloned.1.call-done.refs_0_ = bf16[40,1536,512]{2,1,0:T(8,128)(2,1)} async-done(((bf16[5,1536,512]{2,1,0:T(8,128)(2,1)}), bf16[40,1536,512]{2,1,0:T(8,128)(2,1)}) %all-gather.4.cloned.1.call-update) | async-done | bytes 62914576 | tf_op jit(solution)/shard_map/all_gather | solution.py:204
  291.5 281.3 %all-gather.6.cloned.1.call-done.refs_1_ = bf16[40,1536,512]{2,1,0:T(8,128)(2,1)} async-done(((bf16[5,1536,512]{2,1,0:T(8,128)(2,1)}), bf16[40,1536,512]{2,1,0:T(8,128)(2,1)}) %all-gather.6.cloned.1.call-update) | async-done | bytes 62914576 | tf_op jit(solution)/shard_map/all_gather | solution.py:204
  572.8 281.3 %all-gather.8.cloned.1.call-done.refs_2_ = bf16[40,512,1536]{2,1,0:T(8,128)(2,1)} async-done(((bf16[5,512,1536]{2,1,0:T(8,128)(2,1)}), bf16[40,512,1536]{2,1,0:T(8,128)(2,1)}) %all-gather.8.cloned.1.call-update) | async-done | bytes 62914576 | tf_op jit(solution)/shard_map/all_gather | solution.py:204
  854.1 434.8 %experts_40.1 = bf16[4096,1536]{1,0:T(8,128)(2,1)} custom-call(s32[40]{0:T(128)} %sub.19.starts, s32[40]{0:T(128)} %copy-done.2, s32[33024]{0:T(1024)} %pad.8.address, f32[33024]{0:T(1024)} %pad.9.gates, f32[49152,128]{1,0:T(8,128)} %bitcast.17, bf16[40,1536,512]{2,1,0:T(8,128)(2,1)} %all-gather.4.cloned.1.call-done.refs_0_, ...), custom_call_target="tpu_custom_call" | custom-call | flops 154769817600 | bytes 188743680 | tf_op jit(solution)/shard_map/experts_40/pallas_call | solution.py:173
  (10 shorter events, 0.2 us)
Async XLA Ops:
  6.5 284.9 %all-gather.4.cloned.1.call-start = ((), (), s32[]{:S(2)}) async-start(), calls=%async_computation | async-start | bytes 70778880 | tf_op jit(solution)/shard_map/all_gather | solution.py:204
  7.3 1.5 copy-start
  7.3 3.0 copy-start.1
  7.3 565.5 %all-gather.6.cloned.1.call-start = ((), (), s32[]{:S(2)}) async-start(), calls=%async_computation.1 | async-start | bytes 70778880 | tf_op jit(solution)/shard_map/all_gather | solution.py:204
  8.0 846.0 %all-gather.8.cloned.1.call-start = ((), (), s32[]{:S(2)}) async-start(), calls=%async_computation.2 | async-start | bytes 70778880 | tf_op jit(solution)/shard_map/all_gather | solution.py:204
  9.4 0.9 copy-start.2
Sparse Core Ops, SparseCore 0:
  9.2 282.2 all-gather.3
  293.3 279.4 all-gather.5
  574.6 279.4 all-gather.7

commit v2 on v1

v2 whole, which is shorter than its diff:
```python
import functools

import jax
import jax.numpy as jnp
from jax import lax
from jax.experimental import pallas as pl
from jax.experimental.pallas import tpu as pltpu
from jax.sharding import PartitionSpec as P


LANES = 128
SUBLANES = 8
TILE = 256
COST_FLOPS = 4_000_000_000


def route_lists(tokens, routes, w_router):
    num_tokens, _ = routes.shape
    num_experts = w_router.shape[1]
    chunks = tokens.shape[1] // LANES
    logits = jnp.dot(tokens, w_router, preferred_element_type=jnp.float32).T
    slots = routes.T
    experts = jnp.arange(num_experts, dtype=jnp.int32)
    hit = slots[:, None, :] == experts[None, :, None]
    picked = jnp.sum(jnp.where(hit, logits[None], 0.0), axis=1)
    gates = jax.nn.softmax(picked, axis=0)
    counts = jnp.sum(hit, axis=(0, 2), dtype=jnp.int32)
    starts = jnp.cumsum(counts) - counts
    keys = slots * num_tokens + jnp.arange(num_tokens, dtype=jnp.int32)[None, :]
    keys, gates = lax.sort((keys.reshape(-1), gates.reshape(-1)), num_keys=1, is_stable=False)
    token_at = keys % num_tokens
    address = (token_at // SUBLANES) * (SUBLANES * chunks) + token_at % SUBLANES
    return jnp.pad(address, (0, TILE)), jnp.pad(gates, (0, TILE)), starts, counts


def to_tiles(rows):
    num_rows, width = rows.shape
    tiled = rows.reshape(num_rows // SUBLANES, SUBLANES, width // LANES, LANES)
    return tiled.transpose(0, 2, 1, 3).reshape(num_rows * (width // LANES), LANES)


def pack_kernel(cuts, w_one, w_three, w_two, *refs):
    outs, (buffer, in_sem, out_sem) = refs[:len(cuts)], refs[len(cuts):]
    slots = sorted({s for s, _, _ in cuts})
    d_expert = w_one.shape[2]

    def loads(i, s):
        pairs = [(w_one.at[s], buffer.at[i, 0]), (w_three.at[s], buffer.at[i, 1])]
        for c in range(w_two.shape[2] // d_expert):
            pairs.append((w_two.at[s, :, pl.ds(c * d_expert, d_expert)], buffer.at[i, 2, pl.ds(c * d_expert, d_expert)]))
        return [pltpu.make_async_copy(a, b, in_sem.at[i, j]) for j, (a, b) in enumerate(pairs)]

    stores = [
        pltpu.make_async_copy(buffer.at[slots.index(s), :, pl.ds(row, size)], outs[k], out_sem.at[k])
        for k, (s, row, size) in enumerate(cuts)
    ]
    for i, s in enumerate(slots):
        for copy in loads(i, s):
            copy.start()
    for i, s in enumerate(slots):
        for copy in loads(i, s):
            copy.wait()
        for k, cut in enumerate(cuts):
            if cut[0] == s:
                stores[k].start()
    for copy in stores:
        copy.wait()


def pack(cuts, w_one, w_three, w_two):
    _, d_model, d_expert = w_one.shape
    num_slots = len({s for s, _, _ in cuts})
    return pl.pallas_call(
        functools.partial(pack_kernel, cuts),
        out_shape=[jax.ShapeDtypeStruct((3, size, d_expert), w_one.dtype) for _, _, size in cuts],
        in_specs=[pl.BlockSpec(memory_space=pl.ANY)] * 3,
        out_specs=[pl.BlockSpec(memory_space=pl.ANY)] * len(cuts),
        scratch_shapes=[
            pltpu.VMEM((num_slots, 3, d_model, d_expert), w_one.dtype),
            pltpu.SemaphoreType.DMA((num_slots, 2 + d_model // d_expert)),
            pltpu.SemaphoreType.DMA((len(cuts),)),
        ],
    )(w_one, w_three, w_two)


def stage_kernel(first, last, offset, plan, d_model, d_expert, starts, counts, address, gates, x_hbm, *refs):
    refs = list(refs)
    y_hbm = None if first else refs.pop(0)
    num_arrays = 1 + max(piece[0] for pieces in plan for piece in pieces)
    weights, refs = refs[:num_arrays], refs[num_arrays:]
    out, x_v, y_v, w_v, rows_v, outs_v, cast_v, w_sem, io_sem = refs
    chunks = d_model // LANES
    num_stage = len(plan)

    def start_weights(step):
        slot = lax.rem(step, 2)
        for i, pieces in enumerate(plan):
            @pl.when(step == i)
            def _(pieces=pieces):
                for array, source, target in pieces:
                    pltpu.make_async_copy(weights[array].at[source], w_v.at[(slot,) + target], w_sem.at[slot]).start()

    def wait_weights(step):
        slot = lax.rem(step, 2)
        pltpu.make_async_copy(w_v.at[slot], w_v.at[slot], w_sem.at[slot]).wait()

    x_copy = pltpu.make_async_copy(x_hbm, x_v, io_sem.at[0])
    x_copy.start()
    start_weights(0)
    if first:
        def clear(i, _):
            y_v[pl.ds(pl.multiple_of(i * 256, 256), 256), :] = jnp.zeros((256, LANES), jnp.float32)
            return 0

        lax.fori_loop(0, y_v.shape[0] // 256, clear, 0)
    else:
        y_copy = pltpu.make_async_copy(y_hbm, y_v, io_sem.at[1])
        y_copy.start()
        y_copy.wait()
    x_copy.wait()

    def row_slice(base):
        return pl.ds(base, chunks, stride=SUBLANES)

    def expert(e, _):
        slot = lax.rem(e, 2)
        start_weights(e + 1)
        wait_weights(e)
        begin = starts[offset + e]
        count = counts[offset + e]

        def tile(t, _):
            tile_begin = begin + t * TILE
            live = jnp.minimum(count - t * TILE, TILE)

            def gather(g, _):
                at = tile_begin + g * SUBLANES
                rows = [x_v[row_slice(address[at + u]), :] for u in range(SUBLANES)]
                for u in range(SUBLANES):
                    rows_v[row_slice(g * (SUBLANES * chunks) + u), :] = rows[u]
                return 0

            lax.fori_loop(0, TILE // SUBLANES, gather, 0)
            tiled = rows_v[...].reshape(TILE // SUBLANES, chunks, SUBLANES, LANES)
            lhs = jnp.concatenate([tiled[:, c].reshape(TILE, LANES).astype(jnp.bfloat16) for c in range(chunks)], axis=1)
            gate_pre = jnp.dot(lhs, w_v[slot, 0], preferred_element_type=jnp.float32)
            up_pre = jnp.dot(lhs, w_v[slot, 1], preferred_element_type=jnp.float32)
            hidden = (jax.nn.silu(gate_pre) * up_pre).astype(jnp.bfloat16)
            parts = []
            for c in range(d_model // d_expert):
                down = jnp.dot(hidden, w_v[slot, 2, c * d_expert:(c + 1) * d_expert], preferred_element_type=jnp.float32)
                down = down.astype(jnp.bfloat16).astype(jnp.float32)
                for k in range(d_expert // LANES):
                    parts.append(down[:, k * LANES:(k + 1) * LANES].reshape(TILE // SUBLANES, 1, SUBLANES, LANES))
            outs_v[...] = jnp.concatenate(parts, axis=1).reshape(TILE * chunks, LANES)

            def add_rows(first_row, size, local):
                at = [tile_begin + first_row + u for u in range(size)]
                where = [address[a] for a in at]
                sums = [y_v[row_slice(w), :] for w in where]
                terms = [outs_v[row_slice(local + u), :] * gates[a] for u, a in enumerate(at)]
                for u in range(size):
                    y_v[row_slice(where[u]), :] = sums[u] + terms[u]

            def scatter(g, _):
                add_rows(g * SUBLANES, SUBLANES, g * (SUBLANES * chunks))
                return 0

            full = live // SUBLANES
            lax.fori_loop(0, full, scatter, 0)

            def scatter_one(r, _):
                add_rows(full * SUBLANES + r, 1, full * (SUBLANES * chunks) + r)
                return 0

            lax.fori_loop(0, live - full * SUBLANES, scatter_one, 0)
            return 0

        lax.fori_loop(0, (count + TILE - 1) // TILE, tile, 0)
        return 0

    lax.fori_loop(0, num_stage, expert, 0)

    if last:
        block = cast_v.shape[1]
        steps = (y_v.shape[0] // chunks) // block

        def out_copy(i):
            return pltpu.make_async_copy(cast_v.at[lax.rem(i, 2)], out.at[pl.ds(pl.multiple_of(i * block, block), block)], io_sem.at[lax.rem(i, 2)])

        def finish(i, _):
            @pl.when(i >= 2)
            def _():
                out_copy(i - 2).wait()

            part = y_v[pl.ds(pl.multiple_of(i * (block * chunks), block * chunks), block * chunks), :].reshape(block // SUBLANES, chunks, SUBLANES, LANES)
            cast_v[lax.rem(i, 2)] = jnp.concatenate([part[:, c].reshape(block, LANES).astype(jnp.bfloat16) for c in range(chunks)], axis=1)
            out_copy(i).start()
            return 0

        lax.fori_loop(0, steps, finish, 0)
        out_copy(steps - 2).wait()
        out_copy(steps - 1).wait()
    else:
        out_copy = pltpu.make_async_copy(y_v, out, io_sem.at[0])
        out_copy.start()
        out_copy.wait()


def run_stage(x_tiles, y_tiles, starts, counts, address, gates, offset, entries, shape, last):
    arrays, plan = [], []
    for entry in entries:
        pieces = []
        for array, source, target in entry:
            at = next((i for i, known in enumerate(arrays) if known is array), None)
            if at is None:
                at = len(arrays)
                arrays.append(array)
            pieces.append((at, source, target))
        plan.append(tuple(pieces))
    d_model, d_expert = shape
    chunks = d_model // LANES
    num_rows = x_tiles.shape[0] // chunks
    first = y_tiles is None
    smem = pl.BlockSpec(memory_space=pltpu.SMEM)
    hbm = pl.BlockSpec(memory_space=pl.ANY)
    operands = [x_tiles] + ([] if first else [y_tiles]) + arrays
    if last:
        out_shape = jax.ShapeDtypeStruct((num_rows, d_model), jnp.bfloat16)
    else:
        out_shape = jax.ShapeDtypeStruct(x_tiles.shape, jnp.float32)
    return pl.pallas_call(
        functools.partial(stage_kernel, first, last, offset, tuple(plan), d_model, d_expert),
        out_shape=out_shape,
        in_specs=[smem] * 4 + [hbm] * len(operands),
        out_specs=hbm,
        scratch_shapes=[
            pltpu.VMEM(x_tiles.shape, jnp.float32),
            pltpu.VMEM(x_tiles.shape, jnp.float32),
            pltpu.VMEM((2, 3, d_model, d_expert), jnp.bfloat16),
            pltpu.VMEM((TILE * chunks, LANES), jnp.float32),
            pltpu.VMEM((TILE * chunks, LANES), jnp.float32),
            pltpu.VMEM((2, 64, d_model), jnp.bfloat16),
            pltpu.SemaphoreType.DMA((2,)),
            pltpu.SemaphoreType.DMA((2,)),
        ],
        input_output_aliases={} if first or last else {5: 0},
        compiler_params=pltpu.CompilerParams(vmem_limit_bytes=67_043_328),
        cost_estimate=pl.CostEstimate(flops=len(plan) * COST_FLOPS, bytes_accessed=len(plan) * 6 * d_model * d_expert, transcendentals=0),
    )(starts, counts, address, gates, *operands)


def solution(mesh):
    row_spec = P(("dp", "ep"), None)
    expert_spec = P("ep", None, None)
    size = mesh.shape["ep"]

    def hop(array, mask):
        return lax.ppermute(array, "ep", [(i, i ^ mask) for i in range(size)])

    def device_step(tokens, routes, w_router, *own):
        local, d_model, d_expert = own[0].shape
        half = d_model // 2
        blocks = d_model // d_expert
        here = {}

        def note(mask, w_one, w_three, w_two):
            for s in range(local):
                here[mask, s] = [(w_one, (s,), (0,)), (w_three, (s,), (1,))] + [
                    (w_two, (s, slice(None), pl.ds(c * d_expert, d_expert)), (2, pl.ds(c * d_expert, d_expert))) for c in range(blocks)
                ]

        note(0, *own)
        note(1, *[hop(w, 1) for w in own])

        def arrive(mask, slot, array):
            other = hop(array, 1)
            here[mask, slot] = [(array, (), ())]
            here[mask ^ 1, slot] = [(other, (), ())]
            return array

        def arrive_halves(mask, slot, low, high):
            for m, (a, b) in ((mask, (low, high)), (mask ^ 1, [hop(h, 1) for h in (low, high)])):
                here[m, slot] = [(a, (), (slice(None), pl.ds(0, half))), (b, (), (slice(None), pl.ds(half, half)))]

        tail = local - 1
        (head,) = pack(((0, 0, d_model),), *own)
        rest = pack(((1, 0, d_model),), *own)
        rest = list(rest) + list(pack(tuple((s, 0, d_model) for s in range(2, tail)) + ((tail, 0, half), (tail, half, half)), *own))
        packs = [head] + rest
        from_x, from_y = [], []
        for s in range(tail):
            from_x.append(arrive(2, s, hop(packs[s], 2)))
            from_y.append(arrive(4, s, hop(packs[s], 4)))
        x_low, x_high = [hop(h, 2) for h in packs[tail:]]
        y_low, y_high = [hop(h, 4) for h in packs[tail:]]
        arrive_halves(2, tail, x_low, x_high)
        arrive_halves(4, tail, y_low, y_high)
        for s in range(tail):
            arrive(6, s, hop(from_x[s], 4) if s < tail // 2 else hop(from_y[s], 2))
        arrive_halves(6, tail, hop(x_low, 4), hop(y_high, 2))

        stages = [
            [(m, s) for m in (0, 1) for s in range(local)],
            [(m, s) for s in (0, 1) for m in (2, 4, 3, 5)],
            [(m, s) for s in (2, 3) for m in (2, 4, 3, 5)],
            [(m, 4) for m in (2, 4, 3, 5)],
            [(m, s) for m in (6, 7) for s in (0, 2)],
            [(m, s) for m in (6, 7) for s in (1, 3)],
            [(6, 4), (7, 4)],
        ]
        flat = [entry for stage in stages for entry in stage]
        me = lax.axis_index("ep")
        masks = jnp.array([m for m, _ in flat], jnp.int32)
        slots = jnp.array([s for _, s in flat], jnp.int32)
        order = (me ^ masks) * local + slots
        address, gates, starts, counts = route_lists(tokens, routes, w_router)
        starts, counts = starts[order], counts[order]
        x_tiles = to_tiles(tokens.astype(jnp.float32))
        y, offset = None, 0
        for i, stage in enumerate(stages):
            y = run_stage(x_tiles, y, starts, counts, address, gates, offset, [here[e] for e in stage], (d_model, d_expert), i == len(stages) - 1)
            offset += len(stage)
        return y

    return jax.shard_map(device_step, mesh=mesh, in_specs=(row_spec, row_spec, P(None, None), expert_spec, expert_spec, expert_spec), out_specs=row_spec, check_vma=False)
```

time: 1300 us -> 1370 us (1.054)
  Pallas kernels: 435 us -> 640 us
  waiting for transfers between devices: 812 us -> 648 us
  starting transfers between devices: 0.08 us -> 34.1 us
    all_gather x3 -> x0, waiting for transfers between devices: 810 us -> none  [device_step(): lax.all_gather(w, 'ep', axis=0, tiled=True)]
    ppermute x0 -> x39, waiting for transfers between devices: none -> 648 us  [hop(): return lax.ppermute(array, 'ep', [(i, i ^ mask) for i in range(size)])]
    pallas_call x1 -> x10, Pallas kernels: 435 us -> 640 us  [the longest x7 620 us: run_stage(): pl.pallas_call(functools.partial(stage_kernel, first, last, offset, tuple...]
    ppermute x0 -> x39, starting transfers between devices: none -> 34.1 us  [hop(): return lax.ppermute(array, 'ep', [(i, i ^ mask) for i in range(size)])]
  transfers between devices with their start and end apart: 3 -> 39, of which waited for: 3 -> 9; matrix products, arithmetic and copies ran while one was open for 3% -> 3% of each run, Pallas kernels for 0% -> 42%
where the time goes in v2:
time: 1370 us
  waiting for transfers between devices  648 us (47%)
  Pallas kernels  640 us (47%)
  starting transfers between devices  34.1 us (2%)
  other arithmetic  25 us (2%)
    ppermute x39, waiting for transfers between devices, hop(): return lax.ppermute(array, 'ep', [(i, i ^ mask) for i in range(size)])  648 us
    pallas_call x7, Pallas kernels, run_stage(): pl.pallas_call(functools.partial(stage_kernel, first, last, offset, tuple...  620 us
    ppermute x39, starting transfers between devices, hop(): return lax.ppermute(array, 'ep', [(i, i ^ mask) for i in range(size)])  34.1 us
  transfers between devices with their start and end apart: 39, of which 9 were waited for; matrix products, arithmetic and copies ran while one was open for 3% of the time, Pallas kernels for 42%

profile of v2, /device:TPU:0, one launch (start us, length us, event | category | flops | bytes accessed | tf_op | source)
XLA Modules:
  0.0 1365.3 jit_solution(16202042812781423673)
XLA Ops:
  0.0 10.8 shard_map.86
  10.8 3.3 collective-permute-start.19
  15.6 4.5 shard_map.83
  20.8 4.6 shard_map.84
  27.4 39.1 %collective-permute-done.19.refs_1_ = bf16[3,768,512]{2,1,0:T(8,128)(2,1)} collective-permute-done((bf16[3,768,512]{2,1,0:T(8,128)(2,1)}, bf16[3,768,512]{2,1,0:T(8,128)(2,1)}, u32[]{:S(2)}, u32[]{:S(2)}) %collective-permute-start.19) | collective-permute-done | bytes 2359328 | tf_op jit(solution)/shard_map/ppermute | solution.py:259
  66.5 2.0 collective-permute-start.20
  70.1 248.3 %collective-permute-done.20.refs_2_ = bf16[3,768,512]{2,1,0:T(8,128)(2,1)S(1)} collective-permute-done((bf16[3,768,512]{2,1,0:T(8,128)(2,1)}, bf16[3,768,512]{2,1,0:T(8,128)(2,1)S(1)}, u32[]{:S(2)}, u32[]{:S(2)}) %collective-permute-start.20) | collective-permute-done | bytes 2359328 | tf_op jit(solution)/shard_map/ppermute | solution.py:259
  324.2 99.2 %collective-permute-done.4.refs_2_ = bf16[3,1536,512]{2,1,0:T(8,128)(2,1)} collective-permute-done((bf16[3,1536,512]{2,1,0:T(8,128)(2,1)}, bf16[3,1536,512]{2,1,0:T(8,128)(2,1)}, u32[]{:S(2)}, u32[]{:S(2)}) %collective-permute-start.4) | collective-permute-done | bytes 4718624 | tf_op jit(solution)/shard_map/ppermute | solution.py:259
  423.4 101.1 %collective-permute-done.12.refs_2_ = bf16[3,1536,512]{2,1,0:T(8,128)(2,1)} collective-permute-done((bf16[3,1536,512]{2,1,0:T(8,128)(2,1)}, bf16[3,1536,512]{2,1,0:T(8,128)(2,1)}, u32[]{:S(2)}, u32[]{:S(2)}) %collective-permute-start.12) | collective-permute-done | bytes 4718624 | tf_op jit(solution)/shard_map/ppermute | solution.py:259
  524.5 99.4 %collective-permute-done.16.refs_6_ = bf16[3,1536,512]{2,1,0:T(8,128)(2,1)} collective-permute-done((bf16[3,1536,512]{2,1,0:T(8,128)(2,1)}, bf16[3,1536,512]{2,1,0:T(8,128)(2,1)}, u32[]{:S(2)}, u32[]{:S(2)}) %collective-permute-start.16) | collective-permute-done | bytes 4718624 | tf_op jit(solution)/shard_map/ppermute | solution.py:259
  629.9 35.6 %collective-permute-done.25.refs_7_ = bf16[3,768,512]{2,1,0:T(8,128)(2,1)S(1)} collective-permute-done((bf16[3,768,512]{2,1,0:T(8,128)(2,1)S(1)}, bf16[3,768,512]{2,1,0:T(8,128)(2,1)S(1)}, u32[]{:S(2)}, u32[]{:S(2)}) %collective-permute-start.25) | collective-permute-done | bytes 2359328 | tf_op jit(solution)/shard_map/ppermute | solution.py:259
  665.7 16.2 %collective-permute-done.35.refs_1_ = bf16[3,768,512]{2,1,0:T(8,128)(2,1)S(1)} collective-permute-done((bf16[3,768,512]{2,1,0:T(8,128)(2,1)}, bf16[3,768,512]{2,1,0:T(8,128)(2,1)S(1)}, u32[]{:S(2)}, u32[]{:S(2)}) %collective-permute-start.35) | collective-permute-done | bytes 2359328 | tf_op jit(solution)/shard_map/ppermute | solution.py:259
  683.0 7.0 collective-permute-done.9.refs_7_
  693.7 8.3 fusion.8
  703.9 7.8 sort.15
  719.3 15.0 %bitcast_convert_fusion = f32[512,8,12,128]{3,1,2,0:T(8,128)} fusion(bf16[4096,1536]{1,0:T(8,128)(2,1)} %param.8), kind=kLoop, calls=%fused_computation.2 | loop fusion | flops 6291456 | bytes 37748736 | tf_op jit(solution)/shard_map/reshape | solution.py:39
  735.4 127.1 %shard_map.82.refs_0_ = f32[49152,128]{1,0:T(8,128)} custom-call(s32[40]{0:T(128)} %gather_fusion, s32[40]{0:T(128)} %gather_fusion.1, s32[33024]{0:T(1024)} %pad.8.address, f32[33024]{0:T(1024)} %pad.9.gates, f32[49152,128]{1,0:T(8,128)} %bitcast.17, bf16[5,1536,512]{2,1,0:T(8,128)(2,1)} %w_one.5, bf16[5,1536,512]{2,1,0:T(8,128)(2,1)} %w_three.5, ...), custom_call_target="tpu_custom_call" | custom-call | flops 40000000000 | bytes 47185920 | tf_op jit(solution)/shard_map/pallas_call | solution.py:232
  863.1 105.0 %shard_map.85.refs_0_ = f32[49152,128]{1,0:T(8,128)} custom-call(s32[40]{0:T(128)} %gather_fusion, s32[40]{0:T(128)} %gather_fusion.1, s32[33024]{0:T(1024)} %pad.8.address, f32[33024]{0:T(1024)} %pad.9.gates, f32[49152,128]{1,0:T(8,128)} %bitcast.18, f32[49152,128]{1,0:T(8,128)} %shard_map.82.refs_0_, ...), custom_call_target="tpu_custom_call", output_to_operand_aliasing={{}: (5, {})} | custom-call | flops 32000000000 | bytes 37748736 | tf_op jit(solution)/shard_map/pallas_call | solution.py:232
  968.1 7.7 collective-permute-start.36
  976.4 111.2 %shard_map.87.refs_0_ = f32[49152,128]{1,0:T(8,128)} custom-call(s32[40]{0:T(128)} %gather_fusion, s32[40]{0:T(128)} %gather_fusion.1, s32[33024]{0:T(1024)} %pad.8.address, f32[33024]{0:T(1024)} %pad.9.gates, f32[49152,128]{1,0:T(8,128)} %bitcast.19, f32[49152,128]{1,0:T(8,128)} %shard_map.85.refs_0_, ...), custom_call_target="tpu_custom_call", output_to_operand_aliasing={{}: (5, {})} | custom-call | flops 32000000000 | bytes 37748736 | tf_op jit(solution)/shard_map/pallas_call | solution.py:232
  1087.6 67.5 %shard_map.88.refs_0_ = f32[49152,128]{1,0:T(8,128)} custom-call(s32[40]{0:T(128)} %gather_fusion, s32[40]{0:T(128)} %gather_fusion.1, s32[33024]{0:T(1024)} %pad.8.address, f32[33024]{0:T(1024)} %pad.9.gates, f32[49152,128]{1,0:T(8,128)} %bitcast.20, f32[49152,128]{1,0:T(8,128)} %shard_map.87.refs_0_, ...), custom_call_target="tpu_custom_call", output_to_operand_aliasing={{}: (5, {})} | custom-call | flops 16000000000 | bytes 18874368 | tf_op jit(solution)/shard_map/pallas_call | solution.py:232
  1155.6 73.3 %shard_map.89.refs_0_ = f32[49152,128]{1,0:T(8,128)} custom-call(s32[40]{0:T(128)} %gather_fusion, s32[40]{0:T(128)} %gather_fusion.1, s32[33024]{0:T(1024)} %pad.8.address, f32[33024]{0:T(1024)} %pad.9.gates, f32[49152,128]{1,0:T(8,128)} %bitcast.21, f32[49152,128]{1,0:T(8,128)} %shard_map.88.refs_0_, ...), custom_call_target="tpu_custom_call", output_to_operand_aliasing={{}: (5, {})} | custom-call | flops 16000000000 | bytes 18874368 | tf_op jit(solution)/shard_map/pallas_call | solution.py:232
  1228.9 73.5 %shard_map.90.refs_0_ = f32[49152,128]{1,0:T(8,128)} custom-call(s32[40]{0:T(128)} %gather_fusion, s32[40]{0:T(128)} %gather_fusion.1, s32[33024]{0:T(1024)} %pad.8.address, f32[33024]{0:T(1024)} %pad.9.gates, f32[49152,128]{1,0:T(8,128)} %bitcast.22, f32[49152,128]{1,0:T(8,128)} %shard_map.89.refs_0_, ...), custom_call_target="tpu_custom_call", output_to_operand_aliasing={{}: (5, {})} | custom-call | flops 16000000000 | bytes 18874368 | tf_op jit(solution)/shard_map/pallas_call | solution.py:232
  1302.4 62.7 %shard_map.91 = bf16[4096,1536]{1,0:T(8,128)(2,1)} custom-call(s32[40]{0:T(128)} %gather_fusion, s32[40]{0:T(128)} %gather_fusion.1, s32[33024]{0:T(1024)} %pad.8.address, f32[33024]{0:T(1024)} %pad.9.gates, f32[49152,128]{1,0:T(8,128)} %bitcast.23, f32[49152,128]{1,0:T(8,128)} %shard_map.90.refs_0_, bf16[3,768,512]{2,1,0:T(8,128)(2,1)} %copy-done.4, ...), custom_call_target="tpu_custom_call" | custom-call | flops 8000000000 | bytes 9437184 | tf_op jit(solution)/shard_map/pallas_call | solution.py:232
  (120 shorter events, 34.4 us)
Async XLA Ops:
  20.2 300.2 %collective-permute-start.3 = (bf16[3,1536,512]{2,1,0:T(8,128)(2,1)}, bf16[3,1536,512]{2,1,0:T(8,128)(2,1)}, u32[]{:S(2)}, u32[]{:S(2)}) collective-permute-start(bf16[3,1536,512]{2,1,0:T(8,128)(2,1)} %shard_map.83), channel_id=1, source_target_pairs={{0,2},{1,3},{2,0},{3,1},{4,6},{5,7},{6,4},{7,5}} | collective-permute-start | bytes 14155784 | tf_op jit(solution)/shard_map/ppermute | solution.py:259
  25.4 296.8 %collective-permute-start.7 = (bf16[3,1536,512]{2,1,0:T(8,128)(2,1)}, bf16[3,1536,512]{2,1,0:T(8,128)(2,1)}, u32[]{:S(2)}, u32[]{:S(2)}) collective-permute-start(bf16[3,1536,512]{2,1,0:T(8,128)(2,1)} %shard_map.84), channel_id=1, source_target_pairs={{0,2},{1,3},{2,0},{3,1},{4,6},{5,7},{6,4},{7,5}} | collective-permute-start | bytes 14155784 | tf_op jit(solution)/shard_map/ppermute | solution.py:259
  26.9 296.8 %collective-permute-start.8 = (bf16[3,1536,512]{2,1,0:T(8,128)(2,1)}, bf16[3,1536,512]{2,1,0:T(8,128)(2,1)}, u32[]{:S(2)}, u32[]{:S(2)}) collective-permute-start(bf16[3,1536,512]{2,1,0:T(8,128)(2,1)} %shard_map.84), channel_id=1, source_target_pairs={{0,4},{1,5},{2,6},{3,7},{4,0},{5,1},{6,2},{7,3}} | collective-permute-start | bytes 14155784 | tf_op jit(solution)/shard_map/ppermute | solution.py:259
  66.5 251.8 %collective-permute-start.20 = (bf16[3,768,512]{2,1,0:T(8,128)(2,1)}, bf16[3,768,512]{2,1,0:T(8,128)(2,1)S(1)}, u32[]{:S(2)}, u32[]{:S(2)}) collective-permute-start(bf16[3,768,512]{2,1,0:T(8,128)(2,1)} %get-tuple-element.16), channel_id=1, source_target_pairs={{0,2},{1,3},{2,0},{3,1},{4,6},{5,7},{6,4},{7,5}} | collective-permute-start | bytes 7077896 | tf_op jit(solution)/shard_map/ppermute | solution.py:259
  68.6 251.6 %collective-permute-start.21 = (bf16[3,768,512]{2,1,0:T(8,128)(2,1)}, bf16[3,768,512]{2,1,0:T(8,128)(2,1)S(1)}, u32[]{:S(2)}, u32[]{:S(2)}) collective-permute-start(bf16[3,768,512]{2,1,0:T(8,128)(2,1)} %get-tuple-element.15), channel_id=1, source_target_pairs={{0,4},{1,5},{2,6},{3,7},{4,0},{5,1},{6,2},{7,3}} | collective-permute-start | bytes 7077896 | tf_op jit(solution)/shard_map/ppermute | solution.py:259
  318.4 105.0 %collective-permute-start.4 = (bf16[3,1536,512]{2,1,0:T(8,128)(2,1)}, bf16[3,1536,512]{2,1,0:T(8,128)(2,1)}, u32[]{:S(2)}, u32[]{:S(2)}) collective-permute-start(bf16[3,1536,512]{2,1,0:T(8,128)(2,1)} %shard_map.83), channel_id=1, source_target_pairs={{0,4},{1,5},{2,6},{3,7},{4,0},{5,1},{6,2},{7,3}} | collective-permute-start | bytes 14155784 | tf_op jit(solution)/shard_map/ppermute | solution.py:259
  320.1 204.3 %collective-permute-start.12 = (bf16[3,1536,512]{2,1,0:T(8,128)(2,1)}, bf16[3,1536,512]{2,1,0:T(8,128)(2,1)}, u32[]{:S(2)}, u32[]{:S(2)}) collective-permute-start(bf16[3,1536,512]{2,1,0:T(8,128)(2,1)} %get-tuple-element.13), channel_id=1, source_target_pairs={{0,4},{1,5},{2,6},{3,7},{4,0},{5,1},{6,2},{7,3}} | collective-permute-start | bytes 14155784 | tf_op jit(solution)/shard_map/ppermute | solution.py:259
  320.4 303.5 %collective-permute-start.16 = (bf16[3,1536,512]{2,1,0:T(8,128)(2,1)}, bf16[3,1536,512]{2,1,0:T(8,128)(2,1)}, u32[]{:S(2)}, u32[]{:S(2)}) collective-permute-start(bf16[3,1536,512]{2,1,0:T(8,128)(2,1)} %get-tuple-element.14), channel_id=1, source_target_pairs={{0,4},{1,5},{2,6},{3,7},{4,0},{5,1},{6,2},{7,3}} | collective-permute-start | bytes 14155784 | tf_op jit(solution)/shard_map/ppermute | solution.py:259
  322.2 301.7 %collective-permute-start.11 = (bf16[3,1536,512]{2,1,0:T(8,128)(2,1)}, bf16[3,1536,512]{2,1,0:T(8,128)(2,1)}, u32[]{:S(2)}, u32[]{:S(2)}) collective-permute-start(bf16[3,1536,512]{2,1,0:T(8,128)(2,1)} %get-tuple-element.13), channel_id=1, source_target_pairs={{0,2},{1,3},{2,0},{3,1},{4,6},{5,7},{6,4},{7,5}} | collective-permute-start | bytes 14155784 | tf_op jit(solution)/shard_map/ppermute | solution.py:259
  323.7 300.7 %collective-permute-start.15 = (bf16[3,1536,512]{2,1,0:T(8,128)(2,1)}, bf16[3,1536,512]{2,1,0:T(8,128)(2,1)}, u32[]{:S(2)}, u32[]{:S(2)}) collective-permute-start(bf16[3,1536,512]{2,1,0:T(8,128)(2,1)} %get-tuple-element.14), channel_id=1, source_target_pairs={{0,2},{1,3},{2,0},{3,1},{4,6},{5,7},{6,4},{7,5}} | collective-permute-start | bytes 14155784 | tf_op jit(solution)/shard_map/ppermute | solution.py:259
  423.4 201.1 %collective-permute-start.23 = (bf16[3,768,512]{2,1,0:T(8,128)(2,1)}, bf16[3,768,512]{2,1,0:T(8,128)(2,1)S(1)}, u32[]{:S(2)}, u32[]{:S(2)}) collective-permute-start(bf16[3,768,512]{2,1,0:T(8,128)(2,1)} %collective-permute-done.19.refs_1_), channel_id=1, source_target_pairs={{0,1},{1,0},{2,3},{3,2},{4,5},{5,4},{6,7},{7,6}} | collective-permute-start | bytes 7077896 | tf_op jit(solution)/shard_map/ppermute | solution.py:259
  524.5 100.5 %collective-permute-start.26 = (bf16[3,768,512]{2,1,0:T(8,128)(2,1)S(1)}, bf16[3,768,512]{2,1,0:T(8,128)(2,1)S(1)}, u32[]{:S(2)}, u32[]{:S(2)}) collective-permute-start(bf16[3,768,512]{2,1,0:T(8,128)(2,1)S(1)} %collective-permute-done.22.refs_4_), channel_id=1, source_target_pairs={{0,1},{1,0},{2,3},{3,2},{4,5},{5,4},{6,7},{7,6}} | collective-permute-start | bytes 7077896 | tf_op jit(solution)/shard_map/ppermute | solution.py:259
  716.3 146.2 %collective-permute-start.28 = (bf16[3,1536,512]{2,1,0:T(8,128)(2,1)}, bf16[3,1536,512]{2,1,0:T(8,128)(2,1)}, u32[]{:S(2)}, u32[]{:S(2)}) collective-permute-start(bf16[3,1536,512]{2,1,0:T(8,128)(2,1)} %collective-permute-done.12.refs_2_), channel_id=1, source_target_pairs={{0,2},{1,3},{2,0},{3,1},{4,6},{5,7},{6,4},{7,5}} | collective-permute-start | bytes 14155784 | tf_op jit(solution)/shard_map/ppermute | solution.py:259
  717.8 145.3 %collective-permute-start.27 = (bf16[3,1536,512]{2,1,0:T(8,128)(2,1)}, bf16[3,1536,512]{2,1,0:T(8,128)(2,1)}, u32[]{:S(2)}, u32[]{:S(2)}) collective-permute-start(bf16[3,1536,512]{2,1,0:T(8,128)(2,1)} %collective-permute-done.3.refs_1_), channel_id=1, source_target_pairs={{0,4},{1,5},{2,6},{3,7},{4,0},{5,1},{6,2},{7,3}} | collective-permute-start | bytes 14155784 | tf_op jit(solution)/shard_map/ppermute | solution.py:259
  734.3 241.6 %collective-permute-start.32 = (bf16[3,1536,512]{2,1,0:T(8,128)(2,1)}, bf16[3,1536,512]{2,1,0:T(8,128)(2,1)}, u32[]{:S(2)}, u32[]{:S(2)}) collective-permute-start(bf16[3,1536,512]{2,1,0:T(8,128)(2,1)} %collective-permute-done.16.refs_6_), channel_id=1, source_target_pairs={{0,2},{1,3},{2,0},{3,1},{4,6},{5,7},{6,4},{7,5}} | collective-permute-start | bytes 14155784 | tf_op jit(solution)/shard_map/ppermute | solution.py:259
  734.8 241.2 %collective-permute-start.31 = (bf16[3,1536,512]{2,1,0:T(8,128)(2,1)}, bf16[3,1536,512]{2,1,0:T(8,128)(2,1)}, u32[]{:S(2)}, u32[]{:S(2)}) collective-permute-start(bf16[3,1536,512]{2,1,0:T(8,128)(2,1)} %collective-permute-done.7.refs_5_), channel_id=1, source_target_pairs={{0,4},{1,5},{2,6},{3,7},{4,0},{5,1},{6,2},{7,3}} | collective-permute-start | bytes 14155784 | tf_op jit(solution)/shard_map/ppermute | solution.py:259
  735.3 232.8 %collective-permute-start.17 = (bf16[3,1536,512]{2,1,0:T(8,128)(2,1)}, bf16[3,1536,512]{2,1,0:T(8,128)(2,1)}, u32[]{:S(2)}, u32[]{:S(2)}) collective-permute-start(bf16[3,1536,512]{2,1,0:T(8,128)(2,1)} %collective-permute-done.15.refs_5_), channel_id=1, source_target_pairs={{0,1},{1,0},{2,3},{3,2},{4,5},{5,4},{6,7},{7,6}} | collective-permute-start | bytes 14155784 | tf_op jit(solution)/shard_map/ppermute | solution.py:259
  862.5 292.8 %collective-permute-start.30 = (bf16[3,1536,512]{2,1,0:T(8,128)(2,1)}, bf16[3,1536,512]{2,1,0:T(8,128)(2,1)}, u32[]{:S(2)}, u32[]{:S(2)}) collective-permute-start(bf16[3,1536,512]{2,1,0:T(8,128)(2,1)} %collective-permute-done.28.refs_2_), channel_id=1, source_target_pairs={{0,1},{1,0},{2,3},{3,2},{4,5},{5,4},{6,7},{7,6}} | collective-permute-start | bytes 14155784 | tf_op jit(solution)/shard_map/ppermute | solution.py:259
  863.0 292.6 %collective-permute-start.29 = (bf16[3,1536,512]{2,1,0:T(8,128)(2,1)}, bf16[3,1536,512]{2,1,0:T(8,128)(2,1)}, u32[]{:S(2)}, u32[]{:S(2)}) collective-permute-start(bf16[3,1536,512]{2,1,0:T(8,128)(2,1)} %collective-permute-done.27.refs_1_), channel_id=1, source_target_pairs={{0,1},{1,0},{2,3},{3,2},{4,5},{5,4},{6,7},{7,6}} | collective-permute-start | bytes 14155784 | tf_op jit(solution)/shard_map/ppermute | solution.py:259
  968.1 186.9 %collective-permute-start.36 = (bf16[3,768,512]{2,1,0:T(8,128)(2,1)}, bf16[3,768,512]{2,1,0:T(8,128)(2,1)}, u32[]{:S(2)}, u32[]{:S(2)}) collective-permute-start(bf16[3,768,512]{2,1,0:T(8,128)(2,1)} %copy-done), channel_id=1, source_target_pairs={{0,2},{1,3},{2,0},{3,1},{4,6},{5,7},{6,4},{7,5}} | collective-permute-start | bytes 7077896 | tf_op jit(solution)/shard_map/ppermute | solution.py:259
  975.9 253.0 %collective-permute-start.34 = (bf16[3,1536,512]{2,1,0:T(8,128)(2,1)}, bf16[3,1536,512]{2,1,0:T(8,128)(2,1)}, u32[]{:S(2)}, u32[]{:S(2)}) collective-permute-start(bf16[3,1536,512]{2,1,0:T(8,128)(2,1)} %collective-permute-done.32.refs_2_), channel_id=1, source_target_pairs={{0,1},{1,0},{2,3},{3,2},{4,5},{5,4},{6,7},{7,6}} | collective-permute-start | bytes 14155784 | tf_op jit(solution)/shard_map/ppermute | solution.py:259
  976.1 252.9 %collective-permute-start.33 = (bf16[3,1536,512]{2,1,0:T(8,128)(2,1)}, bf16[3,1536,512]{2,1,0:T(8,128)(2,1)}, u32[]{:S(2)}, u32[]{:S(2)}) collective-permute-start(bf16[3,1536,512]{2,1,0:T(8,128)(2,1)} %collective-permute-done.31.refs_1_), channel_id=1, source_target_pairs={{0,1},{1,0},{2,3},{3,2},{4,5},{5,4},{6,7},{7,6}} | collective-permute-start | bytes 14155784 | tf_op jit(solution)/shard_map/ppermute | solution.py:259
  1155.1 147.3 %collective-permute-start.37 = (bf16[3,768,512]{2,1,0:T(8,128)(2,1)}, bf16[3,768,512]{2,1,0:T(8,128)(2,1)}, u32[]{:S(2)}, u32[]{:S(2)}) collective-permute-start(bf16[3,768,512]{2,1,0:T(8,128)(2,1)} %copy-done.4), channel_id=1, source_target_pairs={{0,1},{1,0},{2,3},{3,2},{4,5},{5,4},{6,7},{7,6}} | collective-permute-start | bytes 7077896 | tf_op jit(solution)/shard_map/ppermute | solution.py:259
  1155.3 147.1 %collective-permute-start.38 = (bf16[3,768,512]{2,1,0:T(8,128)(2,1)}, bf16[3,768,512]{2,1,0:T(8,128)(2,1)}, u32[]{:S(2)}, u32[]{:S(2)}) collective-permute-start(bf16[3,768,512]{2,1,0:T(8,128)(2,1)} %collective-permute-done.36.refs_2_), channel_id=1, source_target_pairs={{0,1},{1,0},{2,3},{3,2},{4,5},{5,4},{6,7},{7,6}} | collective-permute-start | bytes 7077896 | tf_op jit(solution)/shard_map/ppermute | solution.py:259
  (32 other events, 2922.3 us)

commit v3 on v2

v3 whole, which is shorter than its diff:
```python
import functools

import jax
import jax.numpy as jnp
from jax import lax
from jax.experimental import pallas as pl
from jax.experimental.pallas import tpu as pltpu
from jax.sharding import PartitionSpec as P


LANES = 128
SUBLANES = 8
TILE = 256
GROUP = 16
BATCH = 8
PIECE = 4
ALIGN = 1024
LIST = 2048
PARTS = 16
AHEAD = 6
COST_FLOPS = 4_000_000_000


def route_lists(tokens, routes, w_router):
    num_tokens, _ = routes.shape
    num_experts = w_router.shape[1]
    chunks = tokens.shape[1] // LANES
    logits = jnp.dot(tokens, w_router, preferred_element_type=jnp.float32).T
    slots = routes.T
    experts = jnp.arange(num_experts, dtype=jnp.int32)
    hit = slots[:, None, :] == experts[None, :, None]
    picked = jnp.sum(jnp.where(hit, logits[None], 0.0), axis=1)
    gates = jax.nn.softmax(picked, axis=0)
    counts = jnp.sum(hit, axis=(0, 2), dtype=jnp.int32)
    starts = jnp.cumsum(counts) - counts
    keys = slots * num_tokens + jnp.arange(num_tokens, dtype=jnp.int32)[None, :]
    keys, gates = lax.sort((keys.reshape(-1), gates.reshape(-1)), num_keys=1, is_stable=False)
    token_at = keys % num_tokens
    address = token_at * chunks
    return jnp.pad(address, (0, LIST)), jnp.pad(gates, (0, LIST)), starts, counts


def pack_kernel(cuts, w_one, w_three, w_two, *refs):
    outs, (buffer, in_sem, out_sem) = refs[:len(cuts)], refs[len(cuts):]
    slots = sorted({s for s, _, _ in cuts})
    d_expert = w_one.shape[2]

    def loads(i, s):
        pairs = [(w_one.at[s], buffer.at[i, 0]), (w_three.at[s], buffer.at[i, 1])]
        for c in range(w_two.shape[2] // d_expert):
            pairs.append((w_two.at[s, :, pl.ds(c * d_expert, d_expert)], buffer.at[i, 2, pl.ds(c * d_expert, d_expert)]))
        return [pltpu.make_async_copy(a, b, in_sem.at[i, j]) for j, (a, b) in enumerate(pairs)]

    stores = [
        pltpu.make_async_copy(buffer.at[slots.index(s), :, pl.ds(row, size)], outs[k], out_sem.at[k])
        for k, (s, row, size) in enumerate(cuts)
    ]
    for i, s in enumerate(slots):
        for copy in loads(i, s):
            copy.start()
    for i, s in enumerate(slots):
        for copy in loads(i, s):
            copy.wait()
        for k, cut in enumerate(cuts):
            if cut[0] == s:
                stores[k].start()
    for copy in stores:
        copy.wait()


def pack(cuts, w_one, w_three, w_two):
    _, d_model, d_expert = w_one.shape
    num_slots = len({s for s, _, _ in cuts})
    return pl.pallas_call(
        functools.partial(pack_kernel, cuts),
        out_shape=[jax.ShapeDtypeStruct((3, size, d_expert), w_one.dtype) for _, _, size in cuts],
        in_specs=[pl.BlockSpec(memory_space=pl.ANY)] * 3,
        out_specs=[pl.BlockSpec(memory_space=pl.ANY)] * len(cuts),
        scratch_shapes=[
            pltpu.VMEM((num_slots, 3, d_model, d_expert), w_one.dtype),
            pltpu.SemaphoreType.DMA((num_slots, 2 + d_model // d_expert)),
            pltpu.SemaphoreType.DMA((len(cuts),)),
        ],
    )(w_one, w_three, w_two)


def next_tile(counts, e, t):
    more = (t + 1) * TILE < counts[e]
    return jnp.where(more, e, e + 1), jnp.where(more, t + 1, 0)


def part_reach(count, t, margin, entry, part_rows, num_parts):
    full = count - t * TILE >= TILE + margin
    return jnp.where(full, entry // part_rows + 1 - margin, num_parts)


def wait_parts(ready, which, copy, need, num_parts):
    have = ready[which]

    def one(k, _):
        copy(k).wait()

        @pl.when(k + AHEAD < num_parts)
        def _():
            copy(k + AHEAD).start()

        return 0

    lax.fori_loop(have, need, one, 0)
    ready[which] = jnp.maximum(have, need)


def row_pieces(base, chunks):
    return [pl.ds(pl.multiple_of(base + q * PIECE, PIECE), PIECE) for q in range(chunks // PIECE)]


def gather_kernel(num_experts, starts, counts, address, x_hbm, out, x_v, rows_v, tile_v, ready, x_sem, out_sem):
    chunks = tile_v.shape[2] // LANES
    num_parts = x_sem.shape[0]
    part_rows = x_v.shape[0] // num_parts

    def x_copy(k):
        rows = pl.ds(pl.multiple_of(k * part_rows, part_rows), part_rows)
        return pltpu.make_async_copy(x_hbm.at[rows], x_v.at[rows], x_sem.at[k])

    def out_copy(g):
        slot = lax.rem(g, 2)
        return pltpu.make_async_copy(tile_v.at[slot], out.at[g], out_sem.at[slot])

    def start_x(k, _):
        x_copy(k).start()
        return 0

    lax.fori_loop(0, AHEAD, start_x, 0)
    ready[0] = 0

    def tile(carry):
        e, t, g = carry
        at = starts[e] + t * TILE
        wait_parts(ready, 0, x_copy, part_reach(counts[e], t, 0, address[at + TILE - 1], part_rows, num_parts), num_parts)

        def gather_rows(i, _):
            for u in range(GROUP):
                target = i * (GROUP * chunks) + (u // SUBLANES) * (SUBLANES * chunks) + u % SUBLANES
                for q, piece in enumerate(row_pieces(address[at + i * GROUP + u], chunks)):
                    rows_v[pl.ds(target + q * (PIECE * SUBLANES), PIECE, stride=SUBLANES), :] = x_v[piece, :]
            return 0

        lax.fori_loop(0, TILE // GROUP, gather_rows, 0)

        @pl.when(g >= 2)
        def _():
            out_copy(g - 2).wait()

        tiled = rows_v[...].reshape(TILE // SUBLANES, chunks, SUBLANES, LANES)
        tile_v[lax.rem(g, 2)] = jnp.concatenate([tiled[:, c].reshape(TILE, LANES).astype(jnp.bfloat16) for c in range(chunks)], axis=1)
        out_copy(g).start()
        return next_tile(counts, e, t) + (g + 1,)

    g = lax.while_loop(lambda carry: carry[0] < num_experts, tile, (jnp.int32(0),) * 3)[2]
    wait_parts(ready, 0, x_copy, num_parts, num_parts)
    out_copy(g - 2).wait()
    out_copy(g - 1).wait()


def gather_tiles(x_rows, starts, counts, address, num_experts, d_model):
    chunks = d_model // LANES
    num_pairs = address.shape[0] - LIST
    smem = pl.BlockSpec(memory_space=pltpu.SMEM)
    hbm = pl.BlockSpec(memory_space=pl.ANY)
    return pl.pallas_call(
        functools.partial(gather_kernel, num_experts),
        out_shape=jax.ShapeDtypeStruct((num_pairs // TILE + num_experts, TILE, d_model), jnp.bfloat16),
        in_specs=[smem] * 3 + [hbm],
        out_specs=hbm,
        scratch_shapes=[
            pltpu.VMEM(x_rows.shape, jnp.float32),
            pltpu.VMEM((TILE * chunks, LANES), jnp.float32),
            pltpu.VMEM((2, TILE, d_model), jnp.bfloat16),
            pltpu.SMEM((1,), jnp.int32),
            pltpu.SemaphoreType.DMA((PARTS,)),
            pltpu.SemaphoreType.DMA((2,)),
        ],
        compiler_params=pltpu.CompilerParams(vmem_limit_bytes=64 * 2**20 - 2**16),
        cost_estimate=pl.CostEstimate(flops=10 * COST_FLOPS, bytes_accessed=num_pairs * d_model * 2, transcendentals=0),
        name="gather_tiles",
    )(starts, counts, address, x_rows)


def stage_kernel(first, last, offset, plan, d_model, d_expert, starts, counts, address, gates, tiles_hbm, *refs):
    refs = list(refs)
    y_hbm = None if first else refs.pop(0)
    num_arrays = 1 + max(piece[0] for pieces in plan for piece in pieces)
    weights, refs = refs[:num_arrays], refs[num_arrays:]
    out, y_v, w_v, tile_v, outs_v, cast_v, address_s, gates_s, ready, w_sem, tile_sem, list_sem, y_sem, out_sem = refs
    chunks = d_model // LANES
    stop = offset + len(plan)
    num_parts = y_sem.shape[0]
    part_rows = y_v.shape[0] // num_parts

    def part(ref, k):
        return ref.at[pl.ds(pl.multiple_of(k * part_rows, part_rows), part_rows)]

    def start_weights(e):
        slot = lax.rem(e, 2)
        for i, pieces in enumerate(plan):
            @pl.when(e == offset + i)
            def _(pieces=pieces):
                for array, source, target in pieces:
                    pltpu.make_async_copy(weights[array].at[source], w_v.at[(slot,) + target], w_sem.at[slot]).start()

    def wait_weights(e):
        slot = lax.rem(e, 2)
        pltpu.make_async_copy(w_v.at[slot], w_v.at[slot], w_sem.at[slot]).wait()

    def tile_copies(e, t, g):
        slot = lax.rem(g, 2)
        window = pl.multiple_of((starts[e] + t * TILE) // ALIGN * ALIGN, ALIGN)
        held = pl.ds(pl.multiple_of(slot * LIST, LIST), LIST)
        return [
            pltpu.make_async_copy(tiles_hbm.at[g], tile_v.at[slot], tile_sem.at[slot]),
            pltpu.make_async_copy(address.at[pl.ds(window, LIST)], address_s.at[held], list_sem.at[slot, 0]),
            pltpu.make_async_copy(gates.at[pl.ds(window, LIST)], gates_s.at[held], list_sem.at[slot, 1]),
        ]

    def y_copy(k):
        return pltpu.make_async_copy(part(y_hbm, k), part(y_v, k), y_sem.at[k])

    def count_tiles(e, total):
        return total + (counts[e] + TILE - 1) // TILE

    first_tile = lax.fori_loop(0, offset, count_tiles, jnp.int32(0))
    start_weights(jnp.int32(offset))
    for copy in tile_copies(jnp.int32(offset), jnp.int32(0), first_tile):
        copy.start()
    for i in range(2):
        ready[i] = 0
    if first:
        def clear(i, _):
            y_v[pl.ds(pl.multiple_of(i * 256, 256), 256), :] = jnp.zeros((256, LANES), jnp.float32)
            return 0

        lax.fori_loop(0, y_v.shape[0] // 256, clear, 0)
    else:
        def start_y(k, _):
            y_copy(k).start()
            return 0

        lax.fori_loop(0, AHEAD, start_y, 0)

    def add_rows(at, local, size):
        where = [row_pieces(address_s[at + u], chunks) for u in range(size)]
        sums = [[y_v[piece, :] for piece in pieces] for pieces in where]
        for u in range(size):
            gate = gates_s[at + u]
            terms = [outs_v[piece, :] * gate for piece in row_pieces(local + u * chunks, chunks)]
            sums[u] = [a + b for a, b in zip(sums[u], terms)]
        for u in range(size):
            for piece, value in zip(where[u], sums[u]):
                y_v[piece, :] = value

    if last:
        block = cast_v.shape[1]
        block_rows = block * chunks
        per_part = part_rows // block_rows

        def out_copy(i):
            slot = lax.rem(i, 2)
            return pltpu.make_async_copy(cast_v.at[slot], out.at[pl.ds(pl.multiple_of(i * block, block), block)], out_sem.at[slot])

        def store_part(k, _):
            for j in range(per_part):
                i = k * per_part + j

                @pl.when(i >= 2)
                def _():
                    out_copy(i - 2).wait()

                held = [y_v[pl.ds(i * block_rows + c, block, stride=chunks), :] for c in range(chunks)]
                cast_v[lax.rem(i, 2)] = jnp.concatenate([h.astype(jnp.bfloat16) for h in held], axis=1)
                out_copy(i).start()
            return 0
    else:
        def out_copy(k):
            return pltpu.make_async_copy(part(y_v, k), part(out, k), out_sem.at[k])

        def store_part(k, _):
            out_copy(k).start()
            return 0

    def tile(carry):
        e, t, g = carry
        slot = lax.rem(g, 2)
        w_slot = lax.rem(e, 2)
        begin = starts[e]
        count = counts[e]
        next_e, next_t = next_tile(counts, e, t)

        @pl.when(next_e < stop)
        def _():
            for copy in tile_copies(next_e, next_t, g + 1):
                copy.start()

        @pl.when(t == 0)
        def _():
            wait_weights(e)
            start_weights(e + 1)

        for copy in tile_copies(e, t, g):
            copy.wait()
        gate_pre = jnp.dot(tile_v[slot], w_v[w_slot, 0], preferred_element_type=jnp.float32)
        up_pre = jnp.dot(tile_v[slot], w_v[w_slot, 1], preferred_element_type=jnp.float32)
        hidden = (jax.nn.silu(gate_pre) * up_pre).astype(jnp.bfloat16)
        for c in range(d_model // d_expert):
            down = jnp.dot(hidden, w_v[w_slot, 2, c * d_expert:(c + 1) * d_expert], preferred_element_type=jnp.float32)
            down = down.astype(jnp.bfloat16).astype(jnp.float32)
            for k in range(d_expert // LANES):
                outs_v[pl.ds(c * (d_expert // LANES) + k, TILE, stride=chunks), :] = down[:, k * LANES:(k + 1) * LANES]

        here = slot * LIST + lax.rem(begin + t * TILE, ALIGN)
        final = address_s[here + TILE - 1]
        if not first:
            wait_parts(ready, 0, y_copy, part_reach(count, t, 0, final, part_rows, num_parts), num_parts)
        live = jnp.minimum(count - t * TILE, TILE)
        full = live // GROUP

        def add_group(i, _):
            for s in range(0, GROUP, BATCH):
                add_rows(here + i * GROUP + s, (i * GROUP + s) * chunks, BATCH)
            return 0

        def add_one(r, _):
            add_rows(here + r, r * chunks, 1)
            return 0

        lax.fori_loop(0, full, add_group, 0)
        lax.fori_loop(full * GROUP, live, add_one, 0)

        @pl.when(e == stop - 1)
        def _():
            settled = part_reach(count, t, 1, final, part_rows, num_parts)
            lax.fori_loop(ready[1], settled, store_part, 0)
            ready[1] = jnp.maximum(ready[1], settled)

        return next_e, next_t, g + 1

    lax.while_loop(lambda carry: carry[0] < stop, tile, (jnp.int32(offset), jnp.int32(0), first_tile))
    if last:
        num_blocks = (y_v.shape[0] // chunks) // block
        out_copy(num_blocks - 2).wait()
        out_copy(num_blocks - 1).wait()
    else:
        def drain(k, _):
            out_copy(k).wait()
            return 0

        lax.fori_loop(0, num_parts, drain, 0)


def run_stage(tiles, y_rows, num_rows, starts, counts, address, gates, offset, entries, shape, last):
    arrays, plan = [], []
    for entry in entries:
        pieces = []
        for array, source, target in entry:
            at = next((i for i, known in enumerate(arrays) if known is array), None)
            if at is None:
                at = len(arrays)
                arrays.append(array)
            pieces.append((at, source, target))
        plan.append(tuple(pieces))
    d_model, d_expert = shape
    chunks = d_model // LANES
    first = y_rows is None
    y_shape = (num_rows * chunks, LANES)
    smem = pl.BlockSpec(memory_space=pltpu.SMEM)
    hbm = pl.BlockSpec(memory_space=pl.ANY)
    operands = [address, gates, tiles] + ([] if first else [y_rows]) + arrays
    if last:
        out_shape = jax.ShapeDtypeStruct((num_rows, d_model), jnp.bfloat16)
    else:
        out_shape = jax.ShapeDtypeStruct(y_shape, jnp.float32)
    return pl.pallas_call(
        functools.partial(stage_kernel, first, last, offset, tuple(plan), d_model, d_expert),
        out_shape=out_shape,
        in_specs=[smem] * 2 + [hbm] * len(operands),
        out_specs=hbm,
        scratch_shapes=[
            pltpu.VMEM(y_shape, jnp.float32),
            pltpu.VMEM((2, 3, d_model, d_expert), jnp.bfloat16),
            pltpu.VMEM((2, TILE, d_model), jnp.bfloat16),
            pltpu.VMEM((TILE * chunks, LANES), jnp.float32),
            pltpu.VMEM((2, 128, d_model), jnp.bfloat16),
            pltpu.SMEM((2 * LIST,), jnp.int32),
            pltpu.SMEM((2 * LIST,), jnp.float32),
            pltpu.SMEM((2,), jnp.int32),
            pltpu.SemaphoreType.DMA((2,)),
            pltpu.SemaphoreType.DMA((2,)),
            pltpu.SemaphoreType.DMA((2, 2)),
            pltpu.SemaphoreType.DMA((PARTS,)),
            pltpu.SemaphoreType.DMA((PARTS,)),
        ],
        input_output_aliases={} if first or last else {5: 0},
        compiler_params=pltpu.CompilerParams(vmem_limit_bytes=64 * 2**20 - 2**16),
        cost_estimate=pl.CostEstimate(flops=len(plan) * COST_FLOPS, bytes_accessed=len(plan) * 6 * d_model * d_expert, transcendentals=0),
    )(starts, counts, *operands)


def solution(mesh):
    row_spec = P(("dp", "ep"), None)
    expert_spec = P("ep", None, None)
    size = mesh.shape["ep"]

    def hop(array, mask):
        return lax.ppermute(array, "ep", [(i, i ^ mask) for i in range(size)])

    def device_step(tokens, routes, w_router, *own):
        local, d_model, d_expert = own[0].shape
        half = d_model // 2
        blocks = d_model // d_expert
        here = {}

        def note(mask, w_one, w_three, w_two):
            for s in range(local):
                here[mask, s] = [(w_one, (s,), (0,)), (w_three, (s,), (1,))] + [
                    (w_two, (s, slice(None), pl.ds(c * d_expert, d_expert)), (2, pl.ds(c * d_expert, d_expert))) for c in range(blocks)
                ]

        note(0, *own)
        note(1, *[hop(w, 1) for w in own])

        def arrive(mask, slot, array):
            other = hop(array, 1)
            here[mask, slot] = [(array, (), ())]
            here[mask ^ 1, slot] = [(other, (), ())]
            return array

        def arrive_halves(mask, slot, low, high):
            for m, (a, b) in ((mask, (low, high)), (mask ^ 1, [hop(h, 1) for h in (low, high)])):
                here[m, slot] = [(a, (), (slice(None), pl.ds(0, half))), (b, (), (slice(None), pl.ds(half, half)))]

        tail = local - 1
        (head,) = pack(((0, 0, d_model),), *own)
        rest = pack(((1, 0, d_model),), *own)
        rest = list(rest) + list(pack(tuple((s, 0, d_model) for s in range(2, tail)) + ((tail, 0, half), (tail, half, half)), *own))
        packs = [head] + rest
        from_x, from_y = [], []
        for s in range(tail):
            from_x.append(arrive(2, s, hop(packs[s], 2)))
            from_y.append(arrive(4, s, hop(packs[s], 4)))
        x_low, x_high = [hop(h, 2) for h in packs[tail:]]
        y_low, y_high = [hop(h, 4) for h in packs[tail:]]
        arrive_halves(2, tail, x_low, x_high)
        arrive_halves(4, tail, y_low, y_high)
        for s in range(tail):
            arrive(6, s, hop(from_x[s], 4) if s < tail // 2 else hop(from_y[s], 2))
        arrive_halves(6, tail, hop(x_low, 4), hop(y_high, 2))

        stages = [
            [(m, s) for m in (0, 1) for s in range(local)],
            [(m, s) for s in (0, 1) for m in (2, 4, 3, 5)],
            [(m, s) for s in (2, 3) for m in (2, 4, 3, 5)],
            [(m, 4) for m in (2, 4, 3, 5)],
            [(m, s) for m in (6, 7) for s in (0, 2)],
            [(m, s) for m in (6, 7) for s in (1, 3)],
            [(6, 4), (7, 4)],
        ]
        flat = [entry for stage in stages for entry in stage]
        me = lax.axis_index("ep")
        masks = jnp.array([m for m, _ in flat], jnp.int32)
        slots = jnp.array([s for _, s in flat], jnp.int32)
        order = (me ^ masks) * local + slots
        address, gates, starts, counts = route_lists(tokens, routes, w_router)
        starts, counts = jnp.pad(starts[order], (0, 1)), jnp.pad(counts[order], (0, 1))
        x_rows = tokens.astype(jnp.float32).reshape(-1, LANES)
        tiles = gather_tiles(x_rows, starts, counts, address, len(flat), d_model)
        y, offset = None, 0
        for i, stage in enumerate(stages):
            y = run_stage(tiles, y, tokens.shape[0], starts, counts, address, gates, offset, [here[e] for e in stage], (d_model, d_expert), i == len(stages) - 1)
            offset += len(stage)
        return y

    return jax.shard_map(device_step, mesh=mesh, in_specs=(row_spec, row_spec, P(None, None), expert_spec, expert_spec, expert_spec), out_specs=row_spec, check_vma=False)
```

time: 1370 us -> 1210 us (0.88)
  Pallas kernels: 640 us -> 480 us
  local copies, waits for them, and re-layouts: 9.27 us -> 32.1 us
  other arithmetic: 25 us -> 10.4 us
    pallas_call x7, Pallas kernels: 620 us -> 363 us  [run_stage(): pl.pallas_call(functools.partial(stage_kernel, first, last, offset, tuple...]
    pallas_call x0 -> x1, Pallas kernels: none -> 96.6 us  [gather_tiles(): pl.pallas_call(functools.partial(gather_kernel, num_experts), out_shape=j...]
    reshape x0 -> x1, local copies, waits for them, and re-layouts: none -> 25.6 us  [device_step(): x_rows = tokens.astype(jnp.float32).reshape(-1, LANES)]
    reshape x1 -> x0, other arithmetic: 15 us -> none  [to_tiles(): tiled.transpose(0, 2, 1, 3).reshape(num_rows * (width // LANES), LANES)]
  transfers between devices with their start and end apart: 39 -> 39, of which waited for: 9 -> 10; matrix products, arithmetic and copies ran while one was open for 3% -> 4% of each run, Pallas kernels for 42% -> 36%
where the time goes in v3:
time: 1210 us
  waiting for transfers between devices  650 us (54%)
  Pallas kernels  480 us (40%)
  starting transfers between devices  32.9 us (3%)
  local copies, waits for them, and re-layouts  32.1 us (3%)
    ppermute x39, waiting for transfers between devices, hop(): return lax.ppermute(array, 'ep', [(i, i ^ mask) for i in range(size)])  650 us
    pallas_call x7, Pallas kernels, run_stage(): pl.pallas_call(functools.partial(stage_kernel, first, last, offset, tuple...  363 us
    pallas_call x1, Pallas kernels, gather_tiles(): pl.pallas_call(functools.partial(gather_kernel, num_experts), out_shape=j...  96.6 us
    ppermute x39, starting transfers between devices, hop(): return lax.ppermute(array, 'ep', [(i, i ^ mask) for i in range(size)])  32.9 us
    reshape x1, local copies, waits for them, and re-layouts, device_step(): x_rows = tokens.astype(jnp.float32).reshape(-1, LANES)  25.6 us
  transfers between devices with their start and end apart: 39, of which 10 were waited for; matrix products, arithmetic and copies ran while one was open for 4% of the time, Pallas kernels for 36%

profile of v3, /device:TPU:0, one launch (start us, length us, event | category | flops | bytes accessed | tf_op | source)
XLA Modules:
  0.0 1214.0 jit_solution(323486123693716210)
XLA Ops:
  0.0 10.7 shard_map.86
  10.7 3.3 collective-permute-start.19
  15.6 4.5 shard_map.83
  20.7 4.5 shard_map.84
  27.2 39.3 %collective-permute-done.19.refs_1_ = bf16[3,768,512]{2,1,0:T(8,128)(2,1)} collective-permute-done((bf16[3,768,512]{2,1,0:T(8,128)(2,1)}, bf16[3,768,512]{2,1,0:T(8,128)(2,1)}, u32[]{:S(2)}, u32[]{:S(2)}) %collective-permute-start.19) | collective-permute-done | bytes 2359328 | tf_op jit(solution)/shard_map/ppermute | solution.py:414
  70.0 248.3 %collective-permute-done.20.refs_2_ = bf16[3,768,512]{2,1,0:T(8,128)(2,1)S(1)} collective-permute-done((bf16[3,768,512]{2,1,0:T(8,128)(2,1)}, bf16[3,768,512]{2,1,0:T(8,128)(2,1)S(1)}, u32[]{:S(2)}, u32[]{:S(2)}) %collective-permute-start.20) | collective-permute-done | bytes 2359328 | tf_op jit(solution)/shard_map/ppermute | solution.py:414
  324.2 99.2 %collective-permute-done.4.refs_2_ = bf16[3,1536,512]{2,1,0:T(8,128)(2,1)} collective-permute-done((bf16[3,1536,512]{2,1,0:T(8,128)(2,1)}, bf16[3,1536,512]{2,1,0:T(8,128)(2,1)}, u32[]{:S(2)}, u32[]{:S(2)}) %collective-permute-start.4) | collective-permute-done | bytes 4718624 | tf_op jit(solution)/shard_map/ppermute | solution.py:414
  423.3 101.1 %collective-permute-done.12.refs_2_ = bf16[3,1536,512]{2,1,0:T(8,128)(2,1)} collective-permute-done((bf16[3,1536,512]{2,1,0:T(8,128)(2,1)}, bf16[3,1536,512]{2,1,0:T(8,128)(2,1)}, u32[]{:S(2)}, u32[]{:S(2)}) %collective-permute-start.12) | collective-permute-done | bytes 4718624 | tf_op jit(solution)/shard_map/ppermute | solution.py:414
  524.4 99.4 %collective-permute-done.16.refs_6_ = bf16[3,1536,512]{2,1,0:T(8,128)(2,1)} collective-permute-done((bf16[3,1536,512]{2,1,0:T(8,128)(2,1)}, bf16[3,1536,512]{2,1,0:T(8,128)(2,1)}, u32[]{:S(2)}, u32[]{:S(2)}) %collective-permute-start.16) | collective-permute-done | bytes 4718624 | tf_op jit(solution)/shard_map/ppermute | solution.py:414
  624.4 4.2 collective-permute-done.23.refs_5_
  636.8 13.1 %collective-permute-done.25.refs_7_ = bf16[3,768,512]{2,1,0:T(8,128)(2,1)S(1)} collective-permute-done((bf16[3,768,512]{2,1,0:T(8,128)(2,1)S(1)}, bf16[3,768,512]{2,1,0:T(8,128)(2,1)S(1)}, u32[]{:S(2)}, u32[]{:S(2)}) %collective-permute-start.25) | collective-permute-done | bytes 2359328 | tf_op jit(solution)/shard_map/ppermute | solution.py:414
  650.1 38.7 %collective-permute-done.35.refs_1_ = bf16[3,768,512]{2,1,0:T(8,128)(2,1)S(1)} collective-permute-done((bf16[3,768,512]{2,1,0:T(8,128)(2,1)}, bf16[3,768,512]{2,1,0:T(8,128)(2,1)S(1)}, u32[]{:S(2)}, u32[]{:S(2)}) %collective-permute-start.35) | collective-permute-done | bytes 2359328 | tf_op jit(solution)/shard_map/ppermute | solution.py:414
  690.8 25.6 %reshape.51.x_hbm = f32[49152,128]{1,0:T(8,128)} reshape(bf16[4096,1536]{1,0:T(8,128)(2,1)} %param.8) | data formatting | bytes 37748736 | tf_op jit(solution)/shard_map/reshape | solution.py:474
  716.5 8.4 fusion.3
  726.8 8.5 sort.15
  742.3 96.6 %gather_tiles.1.tiles_hbm = bf16[168,256,1536]{2,1,0:T(8,128)(2,1)} custom-call(s32[41]{0:T(128)} %pad.15.starts, s32[41]{0:T(128)} %pad.16.counts, s32[34816]{0:T(1024)} %pad.17.address, f32[49152,128]{1,0:T(8,128)} %reshape.51.x_hbm), custom_call_target="tpu_custom_call" | custom-call | flops 40000000000 | bytes 100663296 | tf_op jit(solution)/shard_map/gather_tiles/pallas_call | solution.py:171
  841.1 79.7 %shard_map.82.refs_0_ = f32[49152,128]{1,0:T(8,128)} custom-call(s32[41]{0:T(128)} %pad.15.starts, s32[41]{0:T(128)} %pad.16.counts, s32[34816]{0:T(1024)} %pad.17.address, f32[34816]{0:T(1024)} %pad.18.gates, bf16[168,256,1536]{2,1,0:T(8,128)(2,1)} %gather_tiles.1.tiles_hbm, bf16[5,1536,512]{2,1,0:T(8,128)(2,1)} %w_one.5, bf16[5,1536,512]{2,1,0:T(8,128)(2,1)} %w_three.5, ...), custom_call_target="tpu_custom_call" | custom-call | flops 40000000000 | bytes 47185920 | tf_op jit(solution)/shard_map/pallas_call | solution.py:382
  921.4 63.5 %shard_map.85.refs_0_ = f32[49152,128]{1,0:T(8,128)} custom-call(s32[41]{0:T(128)} %pad.15.starts, s32[41]{0:T(128)} %pad.16.counts, s32[34816]{0:T(1024)} %pad.17.address, f32[34816]{0:T(1024)} %pad.18.gates, bf16[168,256,1536]{2,1,0:T(8,128)(2,1)} %gather_tiles.1.tiles_hbm, f32[49152,128]{1,0:T(8,128)} %shard_map.82.refs_0_, ...), custom_call_target="tpu_custom_call", output_to_operand_aliasing={{}: (5, {})} | custom-call | flops 32000000000 | bytes 37748736 | tf_op jit(solution)/shard_map/pallas_call | solution.py:382
  984.9 6.2 collective-permute-start.36
  992.9 68.1 %shard_map.87.refs_0_ = f32[49152,128]{1,0:T(8,128)} custom-call(s32[41]{0:T(128)} %pad.15.starts, s32[41]{0:T(128)} %pad.16.counts, s32[34816]{0:T(1024)} %pad.17.address, f32[34816]{0:T(1024)} %pad.18.gates, bf16[168,256,1536]{2,1,0:T(8,128)(2,1)} %gather_tiles.1.tiles_hbm, f32[49152,128]{1,0:T(8,128)} %shard_map.85.refs_0_, ...), custom_call_target="tpu_custom_call", output_to_operand_aliasing={{}: (5, {})} | custom-call | flops 32000000000 | bytes 37748736 | tf_op jit(solution)/shard_map/pallas_call | solution.py:382
  1061.0 37.7 %shard_map.88.refs_0_ = f32[49152,128]{1,0:T(8,128)} custom-call(s32[41]{0:T(128)} %pad.15.starts, s32[41]{0:T(128)} %pad.16.counts, s32[34816]{0:T(1024)} %pad.17.address, f32[34816]{0:T(1024)} %pad.18.gates, bf16[168,256,1536]{2,1,0:T(8,128)(2,1)} %gather_tiles.1.tiles_hbm, f32[49152,128]{1,0:T(8,128)} %shard_map.87.refs_0_, ...), custom_call_target="tpu_custom_call", output_to_operand_aliasing={{}: (5, {})} | custom-call | flops 16000000000 | bytes 18874368 | tf_op jit(solution)/shard_map/pallas_call | solution.py:382
  1099.3 40.3 %shard_map.89.refs_0_ = f32[49152,128]{1,0:T(8,128)} custom-call(s32[41]{0:T(128)} %pad.15.starts, s32[41]{0:T(128)} %pad.16.counts, s32[34816]{0:T(1024)} %pad.17.address, f32[34816]{0:T(1024)} %pad.18.gates, bf16[168,256,1536]{2,1,0:T(8,128)(2,1)} %gather_tiles.1.tiles_hbm, f32[49152,128]{1,0:T(8,128)} %shard_map.88.refs_0_, ...), custom_call_target="tpu_custom_call", output_to_operand_aliasing={{}: (5, {})} | custom-call | flops 16000000000 | bytes 18874368 | tf_op jit(solution)/shard_map/pallas_call | solution.py:382
  1139.6 42.1 %shard_map.90.refs_0_ = f32[49152,128]{1,0:T(8,128)} custom-call(s32[41]{0:T(128)} %pad.15.starts, s32[41]{0:T(128)} %pad.16.counts, s32[34816]{0:T(1024)} %pad.17.address, f32[34816]{0:T(1024)} %pad.18.gates, bf16[168,256,1536]{2,1,0:T(8,128)(2,1)} %gather_tiles.1.tiles_hbm, f32[49152,128]{1,0:T(8,128)} %shard_map.89.refs_0_, ...), custom_call_target="tpu_custom_call", output_to_operand_aliasing={{}: (5, {})} | custom-call | flops 16000000000 | bytes 18874368 | tf_op jit(solution)/shard_map/pallas_call | solution.py:382
  1181.7 32.1 %shard_map.91 = bf16[4096,1536]{1,0:T(8,128)(2,1)} custom-call(s32[41]{0:T(128)} %pad.15.starts, s32[41]{0:T(128)} %pad.16.counts, s32[34816]{0:T(1024)} %pad.17.address, f32[34816]{0:T(1024)} %pad.18.gates, bf16[168,256,1536]{2,1,0:T(8,128)(2,1)} %gather_tiles.1.tiles_hbm, f32[49152,128]{1,0:T(8,128)} %shard_map.90.refs_0_, bf16[3,768,512]{2,1,0:T(8,128)(2,1)} %copy-done.7, ...), custom_call_target="tpu_custom_call" | custom-call | flops 8000000000 | bytes 9437184 | tf_op jit(solution)/shard_map/pallas_call | solution.py:382
  (113 shorter events, 38.4 us)
Async XLA Ops:
  20.1 300.2 %collective-permute-start.3 = (bf16[3,1536,512]{2,1,0:T(8,128)(2,1)}, bf16[3,1536,512]{2,1,0:T(8,128)(2,1)}, u32[]{:S(2)}, u32[]{:S(2)}) collective-permute-start(bf16[3,1536,512]{2,1,0:T(8,128)(2,1)} %shard_map.83), channel_id=1, source_target_pairs={{0,2},{1,3},{2,0},{3,1},{4,6},{5,7},{6,4},{7,5}} | collective-permute-start | bytes 14155784 | tf_op jit(solution)/shard_map/ppermute | solution.py:414
  25.2 296.9 %collective-permute-start.7 = (bf16[3,1536,512]{2,1,0:T(8,128)(2,1)}, bf16[3,1536,512]{2,1,0:T(8,128)(2,1)}, u32[]{:S(2)}, u32[]{:S(2)}) collective-permute-start(bf16[3,1536,512]{2,1,0:T(8,128)(2,1)} %shard_map.84), channel_id=1, source_target_pairs={{0,2},{1,3},{2,0},{3,1},{4,6},{5,7},{6,4},{7,5}} | collective-permute-start | bytes 14155784 | tf_op jit(solution)/shard_map/ppermute | solution.py:414
  26.7 296.9 %collective-permute-start.8 = (bf16[3,1536,512]{2,1,0:T(8,128)(2,1)}, bf16[3,1536,512]{2,1,0:T(8,128)(2,1)}, u32[]{:S(2)}, u32[]{:S(2)}) collective-permute-start(bf16[3,1536,512]{2,1,0:T(8,128)(2,1)} %shard_map.84), channel_id=1, source_target_pairs={{0,4},{1,5},{2,6},{3,7},{4,0},{5,1},{6,2},{7,3}} | collective-permute-start | bytes 14155784 | tf_op jit(solution)/shard_map/ppermute | solution.py:414
  66.5 251.8 %collective-permute-start.20 = (bf16[3,768,512]{2,1,0:T(8,128)(2,1)}, bf16[3,768,512]{2,1,0:T(8,128)(2,1)S(1)}, u32[]{:S(2)}, u32[]{:S(2)}) collective-permute-start(bf16[3,768,512]{2,1,0:T(8,128)(2,1)} %get-tuple-element.16), channel_id=1, source_target_pairs={{0,2},{1,3},{2,0},{3,1},{4,6},{5,7},{6,4},{7,5}} | collective-permute-start | bytes 7077896 | tf_op jit(solution)/shard_map/ppermute | solution.py:414
  68.5 251.6 %collective-permute-start.21 = (bf16[3,768,512]{2,1,0:T(8,128)(2,1)}, bf16[3,768,512]{2,1,0:T(8,128)(2,1)S(1)}, u32[]{:S(2)}, u32[]{:S(2)}) collective-permute-start(bf16[3,768,512]{2,1,0:T(8,128)(2,1)} %get-tuple-element.15), channel_id=1, source_target_pairs={{0,4},{1,5},{2,6},{3,7},{4,0},{5,1},{6,2},{7,3}} | collective-permute-start | bytes 7077896 | tf_op jit(solution)/shard_map/ppermute | solution.py:414
  320.1 204.3 %collective-permute-start.12 = (bf16[3,1536,512]{2,1,0:T(8,128)(2,1)}, bf16[3,1536,512]{2,1,0:T(8,128)(2,1)}, u32[]{:S(2)}, u32[]{:S(2)}) collective-permute-start(bf16[3,1536,512]{2,1,0:T(8,128)(2,1)} %get-tuple-element.13), channel_id=1, source_target_pairs={{0,4},{1,5},{2,6},{3,7},{4,0},{5,1},{6,2},{7,3}} | collective-permute-start | bytes 14155784 | tf_op jit(solution)/shard_map/ppermute | solution.py:414
  320.4 303.5 %collective-permute-start.16 = (bf16[3,1536,512]{2,1,0:T(8,128)(2,1)}, bf16[3,1536,512]{2,1,0:T(8,128)(2,1)}, u32[]{:S(2)}, u32[]{:S(2)}) collective-permute-start(bf16[3,1536,512]{2,1,0:T(8,128)(2,1)} %get-tuple-element.14), channel_id=1, source_target_pairs={{0,4},{1,5},{2,6},{3,7},{4,0},{5,1},{6,2},{7,3}} | collective-permute-start | bytes 14155784 | tf_op jit(solution)/shard_map/ppermute | solution.py:414
  322.1 301.7 %collective-permute-start.11 = (bf16[3,1536,512]{2,1,0:T(8,128)(2,1)}, bf16[3,1536,512]{2,1,0:T(8,128)(2,1)}, u32[]{:S(2)}, u32[]{:S(2)}) collective-permute-start(bf16[3,1536,512]{2,1,0:T(8,128)(2,1)} %get-tuple-element.13), channel_id=1, source_target_pairs={{0,2},{1,3},{2,0},{3,1},{4,6},{5,7},{6,4},{7,5}} | collective-permute-start | bytes 14155784 | tf_op jit(solution)/shard_map/ppermute | solution.py:414
  323.6 300.7 %collective-permute-start.15 = (bf16[3,1536,512]{2,1,0:T(8,128)(2,1)}, bf16[3,1536,512]{2,1,0:T(8,128)(2,1)}, u32[]{:S(2)}, u32[]{:S(2)}) collective-permute-start(bf16[3,1536,512]{2,1,0:T(8,128)(2,1)} %get-tuple-element.14), channel_id=1, source_target_pairs={{0,2},{1,3},{2,0},{3,1},{4,6},{5,7},{6,4},{7,5}} | collective-permute-start | bytes 14155784 | tf_op jit(solution)/shard_map/ppermute | solution.py:414
  423.3 265.6 %collective-permute-start = (bf16[5,1536,512]{2,1,0:T(8,128)(2,1)}, bf16[5,1536,512]{2,1,0:T(8,128)(2,1)}, u32[]{:S(2)}, u32[]{:S(2)}) collective-permute-start(bf16[5,1536,512]{2,1,0:T(8,128)(2,1)} %w_one.5), channel_id=1, source_target_pairs={{0,1},{1,0},{2,3},{3,2},{4,5},{5,4},{6,7},{7,6}} | collective-permute-start | bytes 23592968 | tf_op jit(solution)/shard_map/ppermute | solution.py:414
  524.4 165.9 %collective-permute-start.1 = (bf16[5,1536,512]{2,1,0:T(8,128)(2,1)}, bf16[5,1536,512]{2,1,0:T(8,128)(2,1)}, u32[]{:S(2)}, u32[]{:S(2)}) collective-permute-start(bf16[5,1536,512]{2,1,0:T(8,128)(2,1)} %w_three.5), channel_id=1, source_target_pairs={{0,1},{1,0},{2,3},{3,2},{4,5},{5,4},{6,7},{7,6}} | collective-permute-start | bytes 23592968 | tf_op jit(solution)/shard_map/ppermute | solution.py:414
  628.6 106.6 %collective-permute-start.2 = (bf16[5,512,1536]{2,1,0:T(8,128)(2,1)}, bf16[5,512,1536]{2,1,0:T(8,128)(2,1)}, u32[]{:S(2)}, u32[]{:S(2)}) collective-permute-start(bf16[5,512,1536]{2,1,0:T(8,128)(2,1)} %w_two.5), channel_id=1, source_target_pairs={{0,1},{1,0},{2,3},{3,2},{4,5},{5,4},{6,7},{7,6}} | collective-permute-start | bytes 23592968 | tf_op jit(solution)/shard_map/ppermute | solution.py:414
  735.2 105.8 %collective-permute-start.18 = (bf16[3,1536,512]{2,1,0:T(8,128)(2,1)}, bf16[3,1536,512]{2,1,0:T(8,128)(2,1)}, u32[]{:S(2)}, u32[]{:S(2)}) collective-permute-start(bf16[3,1536,512]{2,1,0:T(8,128)(2,1)} %collective-permute-done.16.refs_6_), channel_id=1, source_target_pairs={{0,1},{1,0},{2,3},{3,2},{4,5},{5,4},{6,7},{7,6}} | collective-permute-start | bytes 14155784 | tf_op jit(solution)/shard_map/ppermute | solution.py:414
  735.7 105.3 %collective-permute-start.13 = (bf16[3,1536,512]{2,1,0:T(8,128)(2,1)}, bf16[3,1536,512]{2,1,0:T(8,128)(2,1)}, u32[]{:S(2)}, u32[]{:S(2)}) collective-permute-start(bf16[3,1536,512]{2,1,0:T(8,128)(2,1)} %collective-permute-done.11.refs_1_), channel_id=1, source_target_pairs={{0,1},{1,0},{2,3},{3,2},{4,5},{5,4},{6,7},{7,6}} | collective-permute-start | bytes 14155784 | tf_op jit(solution)/shard_map/ppermute | solution.py:414
  739.3 181.5 %collective-permute-start.28 = (bf16[3,1536,512]{2,1,0:T(8,128)(2,1)}, bf16[3,1536,512]{2,1,0:T(8,128)(2,1)}, u32[]{:S(2)}, u32[]{:S(2)}) collective-permute-start(bf16[3,1536,512]{2,1,0:T(8,128)(2,1)} %collective-permute-done.12.refs_2_), channel_id=1, source_target_pairs={{0,2},{1,3},{2,0},{3,1},{4,6},{5,7},{6,4},{7,5}} | collective-permute-start | bytes 14155784 | tf_op jit(solution)/shard_map/ppermute | solution.py:414
  740.8 180.5 %collective-permute-start.27 = (bf16[3,1536,512]{2,1,0:T(8,128)(2,1)}, bf16[3,1536,512]{2,1,0:T(8,128)(2,1)}, u32[]{:S(2)}, u32[]{:S(2)}) collective-permute-start(bf16[3,1536,512]{2,1,0:T(8,128)(2,1)} %collective-permute-done.3.refs_1_), channel_id=1, source_target_pairs={{0,4},{1,5},{2,6},{3,7},{4,0},{5,1},{6,2},{7,3}} | collective-permute-start | bytes 14155784 | tf_op jit(solution)/shard_map/ppermute | solution.py:414
  840.5 150.5 %collective-permute-start.32 = (bf16[3,1536,512]{2,1,0:T(8,128)(2,1)}, bf16[3,1536,512]{2,1,0:T(8,128)(2,1)}, u32[]{:S(2)}, u32[]{:S(2)}) collective-permute-start(bf16[3,1536,512]{2,1,0:T(8,128)(2,1)} %collective-permute-done.16.refs_6_), channel_id=1, source_target_pairs={{0,2},{1,3},{2,0},{3,1},{4,6},{5,7},{6,4},{7,5}} | collective-permute-start | bytes 14155784 | tf_op jit(solution)/shard_map/ppermute | solution.py:414
  841.1 151.8 %collective-permute-start.31 = (bf16[3,1536,512]{2,1,0:T(8,128)(2,1)}, bf16[3,1536,512]{2,1,0:T(8,128)(2,1)}, u32[]{:S(2)}, u32[]{:S(2)}) collective-permute-start(bf16[3,1536,512]{2,1,0:T(8,128)(2,1)} %collective-permute-done.7.refs_5_), channel_id=1, source_target_pairs={{0,4},{1,5},{2,6},{3,7},{4,0},{5,1},{6,2},{7,3}} | collective-permute-start | bytes 14155784 | tf_op jit(solution)/shard_map/ppermute | solution.py:414
  841.1 143.8 %collective-permute-start.17 = (bf16[3,1536,512]{2,1,0:T(8,128)(2,1)}, bf16[3,1536,512]{2,1,0:T(8,128)(2,1)}, u32[]{:S(2)}, u32[]{:S(2)}) collective-permute-start(bf16[3,1536,512]{2,1,0:T(8,128)(2,1)} %collective-permute-done.15.refs_5_), channel_id=1, source_target_pairs={{0,1},{1,0},{2,3},{3,2},{4,5},{5,4},{6,7},{7,6}} | collective-permute-start | bytes 14155784 | tf_op jit(solution)/shard_map/ppermute | solution.py:414
  920.8 177.9 %collective-permute-start.30 = (bf16[3,1536,512]{2,1,0:T(8,128)(2,1)}, bf16[3,1536,512]{2,1,0:T(8,128)(2,1)}, u32[]{:S(2)}, u32[]{:S(2)}) collective-permute-start(bf16[3,1536,512]{2,1,0:T(8,128)(2,1)} %collective-permute-done.28.refs_2_), channel_id=1, source_target_pairs={{0,1},{1,0},{2,3},{3,2},{4,5},{5,4},{6,7},{7,6}} | collective-permute-start | bytes 14155784 | tf_op jit(solution)/shard_map/ppermute | solution.py:414
  921.3 177.9 %collective-permute-start.29 = (bf16[3,1536,512]{2,1,0:T(8,128)(2,1)}, bf16[3,1536,512]{2,1,0:T(8,128)(2,1)}, u32[]{:S(2)}, u32[]{:S(2)}) collective-permute-start(bf16[3,1536,512]{2,1,0:T(8,128)(2,1)} %collective-permute-done.27.refs_1_), channel_id=1, source_target_pairs={{0,1},{1,0},{2,3},{3,2},{4,5},{5,4},{6,7},{7,6}} | collective-permute-start | bytes 14155784 | tf_op jit(solution)/shard_map/ppermute | solution.py:414
  984.9 113.8 %collective-permute-start.36 = (bf16[3,768,512]{2,1,0:T(8,128)(2,1)}, bf16[3,768,512]{2,1,0:T(8,128)(2,1)}, u32[]{:S(2)}, u32[]{:S(2)}) collective-permute-start(bf16[3,768,512]{2,1,0:T(8,128)(2,1)} %copy-done), channel_id=1, source_target_pairs={{0,2},{1,3},{2,0},{3,1},{4,6},{5,7},{6,4},{7,5}} | collective-permute-start | bytes 7077896 | tf_op jit(solution)/shard_map/ppermute | solution.py:414
  991.0 148.6 %collective-permute-start.34 = (bf16[3,1536,512]{2,1,0:T(8,128)(2,1)}, bf16[3,1536,512]{2,1,0:T(8,128)(2,1)}, u32[]{:S(2)}, u32[]{:S(2)}) collective-permute-start(bf16[3,1536,512]{2,1,0:T(8,128)(2,1)} %collective-permute-done.32.refs_2_), channel_id=1, source_target_pairs={{0,1},{1,0},{2,3},{3,2},{4,5},{5,4},{6,7},{7,6}} | collective-permute-start | bytes 14155784 | tf_op jit(solution)/shard_map/ppermute | solution.py:414
  992.9 146.7 %collective-permute-start.33 = (bf16[3,1536,512]{2,1,0:T(8,128)(2,1)}, bf16[3,1536,512]{2,1,0:T(8,128)(2,1)}, u32[]{:S(2)}, u32[]{:S(2)}) collective-permute-start(bf16[3,1536,512]{2,1,0:T(8,128)(2,1)} %collective-permute-done.31.refs_1_), channel_id=1, source_target_pairs={{0,1},{1,0},{2,3},{3,2},{4,5},{5,4},{6,7},{7,6}} | collective-permute-start | bytes 14155784 | tf_op jit(solution)/shard_map/ppermute | solution.py:414
  (27 other events, 2298.0 us)
